TPU v7x, 32 devices: a whole 2x2x4 slice. The times are simulated.
32 devices in a mesh: ocn: 4 (over z), grp: 8 (over y, x, core).
Axes of the slice: x: 2, y: 2, z: 4, core: 2. Of those that a mesh axis runs over, the one named last changes fastest.
Arguments:
- tracers: float32 [2, 32, 256, 1024], P(None, None, 'grp', 'ocn'), may hold values from -6 to 6
- velocity: float32 [2, 32, 256, 1024], P(None, None, 'grp', 'ocn'), may hold values from -3 to 3
- remap_weights: bfloat16 [256, 8, 128, 128], P('grp'), may hold values from -0.25 to 0.25
- remap_blocks: int32 [256, 8], P('grp'), may hold values from 0 to 2047
- remap_count: int32 [256], P('grp'), may hold values from 1 to 8, as said below
- ice_velocity: float32 [2, 32768], P(None, 'grp'), may hold values from -3 to 3
- ice_mass_rate: float32 [32768], P('grp'), may hold values from 0.5 to 4
- ice_strength: float32 [32768], P('grp'), may hold values from 0.5 to 8
- wind_stress: float32 [2, 32768], P(None, 'grp'), may hold values from -6 to 6
Outputs:
- tracers_next: float32 [2, 32, 256, 1024], P(None, None, 'grp', 'ocn')
- surface_flux: float32 [3, 256, 1024], P(None, 'grp', 'ocn')
- ice_final: float32 [2, 32768], P(None, 'grp')
Inputs may be any that keep to these rules, and one draw needn't show every extreme that they name: `remap_count`: every ice block has at least one live entry. The ice blocks of the first and of the last index of grp have 7 or 8 live entries; all others have 1 or 2.
All inputs are finite; a program needn't handle non-finite values.
Results may differ from a plain program's by a relative error of at most 0.0006.
The roundings to bfloat16 on the way count: a program that leaves them out, or rounds other values in their place, can miss the bound.
Values may be sent and summed in bfloat16 or wider, within the bound.
No kernel may reach another device: no remote copies, remote signals or barrier semaphores. Data moves between devices by JAX's collectives and lax.ppermute only.
A program may use at most 128 MiB of HBM per device.

v0:
```python
import jax
import jax.numpy as jnp
from jax import lax
from jax.experimental import pallas as pl
from jax.experimental.pallas import tpu as pltpu
from jax.sharding import PartitionSpec as P


BS = 128
ITERS = 4
DEPTH = 3
UNROLL = 8
FWD_SLOTS = 32
BWD_SLOTS = 64
F32 = jnp.float32
BF16 = jnp.bfloat16


VM = pl.BlockSpec(memory_space=pltpu.VMEM)
SM = pl.BlockSpec(memory_space=pltpu.SMEM)
ANY = pl.BlockSpec(memory_space=pl.ANY)


def params(**kw):
    return pltpu.CompilerParams(vmem_limit_bytes=48 * 1024 * 1024, **kw)


def surface_kernel(t_ref, v_ref, out_ref):
    height, across = t_ref.shape[2], t_ref.shape[3]
    for f in range(4):
        src = t_ref if f < 2 else v_ref
        for h in range(across // BS):
            out_ref[f, h * height : (h + 1) * height, :] = src[
                f % 2, 0, :, h * BS : (h + 1) * BS
            ].astype(BF16)


def pack_surface(tracers, velocity):
    height, across = tracers.shape[2:]
    spec = pl.BlockSpec((2, 1, height, across), lambda i: (0, 0, 0, 0))
    nbl = height * across // BS
    return pl.pallas_call(
        surface_kernel,
        grid=(1,),
        in_specs=[spec, spec],
        out_specs=pl.BlockSpec((4, nbl, BS), lambda i: (0, 0, 0)),
        out_shape=jax.ShapeDtypeStruct((4, nbl, BS), BF16),
        name="surface",
    )(tracers, velocity)


def edges_kernel(t_ref, row0_ref, rown_ref, col0_ref, coln_ref):
    step = pl.program_id(0)
    lc, height, across = t_ref.shape[1:]
    levels = lc * pl.num_programs(0)
    lane = lax.broadcasted_iota(jnp.int32, (height, BS), 1)

    @pl.when(step == 0)
    def _():
        col0_ref[...] = jnp.zeros_like(col0_ref)
        coln_ref[...] = jnp.zeros_like(coln_ref)

    first = col0_ref[...]
    last = coln_ref[...]
    for t in range(2):
        for i in range(lc):
            c = t * levels + step * lc + i
            first = jnp.where(lane == c, pltpu.roll(t_ref[t, i, :, :BS], c, 1), first)
            last = jnp.where(
                lane == c, pltpu.roll(t_ref[t, i, :, across - BS :], (c + 1) % BS, 1), last
            )
            row0_ref[t, i : i + 1, :] = t_ref[t, i, 0:1, :]
            rown_ref[t, i : i + 1, :] = t_ref[t, i, height - 1 : height, :]
    col0_ref[...] = first
    coln_ref[...] = last


def pack_edges(tracers):
    _, levels, height, across = tracers.shape
    lc = 8
    rows = jax.ShapeDtypeStruct((2, levels, across), F32)
    cols = jax.ShapeDtypeStruct((height, BS), F32)
    row_spec = pl.BlockSpec((2, lc, across), lambda i: (0, i, 0))
    col_spec = pl.BlockSpec((height, BS), lambda i: (0, 0))
    return pl.pallas_call(
        edges_kernel,
        grid=(levels // lc,),
        in_specs=[pl.BlockSpec((2, lc, height, across), lambda i: (0, i, 0, 0))],
        out_specs=[row_spec, row_spec, col_spec, col_spec],
        out_shape=[rows, rows, cols, cols],
        name="edges",
    )(tracers)


def stencil_kernel(t_ref, up_ref, dn_ref, v_ref, north_ref, south_ref, east_ref, west_ref, out_ref):
    step = pl.program_id(0)
    steps = pl.num_programs(0)
    lc, height, across = t_ref.shape[1:]
    levels = lc * steps
    lane = lax.broadcasted_iota(jnp.int32, (height, across), 1)
    row = lax.broadcasted_iota(jnp.int32, (height, across), 0)
    pad = jnp.zeros((height, across - BS), F32)
    top = jnp.where(step == 0, 0.0, 1.0)
    bottom = jnp.where(step == steps - 1, 0.0, 1.0)
    for i in range(lc):
        u = v_ref[0, i]
        v = v_ref[1, i]
        for t in range(2):
            c = t * levels + step * lc + i
            x = t_ref[t, i]
            above = up_ref[t, 0] * top if i == 0 else t_ref[t, i - 1]
            below = dn_ref[t, 0] * bottom if i == lc - 1 else t_ref[t, i + 1]
            wcol = jnp.concatenate(
                [pltpu.roll(west_ref[...], (BS - c) % BS, 1), pad], axis=1
            )
            ecol = jnp.concatenate([pad, pltpu.roll(east_ref[...], BS - 1 - c, 1)], axis=1)
            w = jnp.where(lane == 0, wcol, pltpu.roll(x, 1, 1))
            e = jnp.where(lane == across - 1, ecol, pltpu.roll(x, across - 1, 1))
            s = jnp.where(row == 0, south_ref[t, i : i + 1, :], pltpu.roll(x, 1, 0))
            n = jnp.where(row == height - 1, north_ref[t, i : i + 1, :], pltpu.roll(x, height - 1, 0))
            advect = u * (e - w) * 0.5 + v * (n - s) * 0.5
            out_ref[t, i] = (
                x
                + 0.2 * (e + w + n + s - 4.0 * x)
                - 0.5 * advect
                + 0.2 * (above + below - 2.0 * x)
            )


def stencil(tracers, velocity, north, south, east, west):
    _, levels, height, across = tracers.shape
    lc = 8
    main = pl.BlockSpec((2, lc, height, across), lambda i: (0, i, 0, 0))
    up = pl.BlockSpec((2, 1, height, across), lambda i: (0, jnp.maximum(i * lc - 1, 0), 0, 0))
    dn = pl.BlockSpec(
        (2, 1, height, across), lambda i: (0, jnp.minimum(i * lc + lc, levels - 1), 0, 0)
    )
    row_spec = pl.BlockSpec((2, lc, across), lambda i: (0, i, 0))
    col_spec = pl.BlockSpec((height, BS), lambda i: (0, 0))
    return pl.pallas_call(
        stencil_kernel,
        grid=(levels // lc,),
        in_specs=[main, up, dn, main, row_spec, row_spec, col_spec, col_spec],
        out_specs=main,
        out_shape=jax.ShapeDtypeStruct(tracers.shape, F32),
        cost_estimate=pl.CostEstimate(
            flops=120_000_000, bytes_accessed=4 * tracers.size * 4, transcendentals=0
        ),
        name="stencil",
    )(tracers, tracers, tracers, velocity, north, south, east, west)


def stream_weights(list_ref, groups, w_hbm, buf, sems, compute):
    slots = buf.shape[0]

    def copy(i, slot):
        return pltpu.make_async_copy(w_hbm.at[list_ref[i]], buf.at[slot], sems.at[slot])

    def start():
        for s in range(slots // UNROLL):

            @pl.when(s < groups)
            def _():
                for q in range(UNROLL):
                    copy(s * UNROLL + q, s * UNROLL + q).start()

    def loop():
        def body(g, carry):
            base = g * UNROLL
            slot = lax.rem(g, slots // UNROLL) * UNROLL
            for q in range(UNROLL):
                copy(base + q, slot + q).wait()
            compute(base, slot)

            @pl.when(g + slots // UNROLL < groups)
            def _():
                for q in range(UNROLL):
                    copy(base + slots + q, slot + q).start()

            return carry

        lax.fori_loop(0, groups, body, 0)

    return start, loop


def forward_kernel(code_ref, surf_ref, w_hbm, out_ref, list_ref, rows, acc, buf, sems):
    entries = code_ref.shape[0]
    ice = acc.shape[0]
    per_block = entries // ice
    nbl = surf_ref.shape[1]

    def scan(i, n):
        for q in range(8):
            e = i * 8 + q
            list_ref[n] = e
            n = n + jnp.where(code_ref[e] >= 0, 1, 0)
        return n

    count = lax.fori_loop(0, entries // 8, scan, 0)
    for q in range(UNROLL):
        list_ref[count + q] = 0
    list_ref[entries + UNROLL] = count
    groups = lax.div(count + UNROLL - 1, UNROLL)
    first = lax.broadcasted_iota(jnp.int32, (4, BS), 0)

    def compute(base, slot):
        for q in range(UNROLL):
            e = list_ref[base + q]
            at = jnp.maximum(code_ref[e], 0)
            r0 = jnp.broadcast_to(rows[pl.ds(at, 1), :], (4, BS))
            r1 = jnp.broadcast_to(rows[pl.ds(at + nbl, 1), :], (4, BS))
            r2 = jnp.broadcast_to(rows[pl.ds(at + 2 * nbl, 1), :], (4, BS))
            r3 = jnp.broadcast_to(rows[pl.ds(at + 3 * nbl, 1), :], (4, BS))
            s = jnp.where(first == 0, r0, jnp.where(first == 1, r1, jnp.where(first == 2, r2, r3)))
            s = jnp.where(base + q < count, s, 0.0).astype(BF16)
            part = lax.dot_general(
                s, buf[slot + q], (((1,), (1,)), ((), ())), preferred_element_type=F32
            )
            r = lax.div(e, per_block)
            acc[r] = acc[r] + part

    start, loop = stream_weights(list_ref, groups, w_hbm, buf, sems, compute)
    start()
    planes = surf_ref.shape[0]
    for p in range(planes):
        rows[p * nbl : (p + 1) * nbl, :] = surf_ref[p].astype(F32)
    acc[...] = jnp.zeros_like(acc)
    loop()
    for r in range(ice):
        a = acc[r]
        out_ref[0, r : r + 1, :] = 0.5 * (-0.05 * a[1:2] - a[0:1])
        out_ref[1, r : r + 1, :] = a[2:3]
        out_ref[2, r : r + 1, :] = a[3:4]


def forward(code, surf, weights, ice):
    entries = weights.shape[0]
    planes, nbl = surf.shape[:2]
    return pl.pallas_call(
        forward_kernel,
        in_specs=[SM, VM, ANY],
        out_specs=[VM, SM],
        out_shape=[
            jax.ShapeDtypeStruct((3, ice, BS), F32),
            jax.ShapeDtypeStruct((entries + UNROLL + 8,), jnp.int32),
        ],
        scratch_shapes=[
            pltpu.VMEM((planes * nbl, BS), F32),
            pltpu.VMEM((ice, 4, BS), F32),
            pltpu.VMEM((FWD_SLOTS, BS, BS), BF16),
            pltpu.SemaphoreType.DMA((FWD_SLOTS,)),
        ],
        compiler_params=params(),
        name="forward",
    )(code, surf, weights)


def combine_kernel(*refs):
    parts = refs[:-6]
    u_ref, wind_ref, rate_ref, strength_ref, x_ref, rem_ref = refs[-6:]
    vals = [p[...] for p in parts]
    while len(vals) > 1:
        vals = [a + b for a, b in zip(vals[0::2], vals[1::2])]
    rem_ref[...] = vals[0]
    ice = rate_ref.shape[0]
    for r in range(ice):
        for c in range(2):
            u = u_ref[c : c + 1, r * BS : (r + 1) * BS]
            x_ref[2 + c, r : r + 1, :] = u
            x_ref[c, r : r + 1, :] = wind_ref[c : c + 1, r * BS : (r + 1) * BS]
    rate = rate_ref[...]
    for c in range(2):
        x_ref[c] = rate * x_ref[2 + c] + x_ref[c] + rem_ref[1 + c]
    x_ref[4] = rate
    x_ref[5] = strength_ref[...]


def combine(parts, u, wind, rate, strength):
    ice = rate.shape[0]
    return pl.pallas_call(
        combine_kernel,
        in_specs=[VM] * (len(parts) + 4),
        out_specs=[VM, VM],
        out_shape=[
            jax.ShapeDtypeStruct((6, ice, BS), F32),
            jax.ShapeDtypeStruct((3, ice, BS), F32),
        ],
        name="combine",
    )(*parts, u, wind, rate, strength)


def solve_kernel(dst_ref, list_ref, me_ref, x_ref, rem_ref, w_hbm, *refs):
    groups_n, _, ice, _ = x_ref.shape
    outs = refs[:groups_n]
    ice_ref, fin, flux, back, buf, sems = refs[groups_n:]
    entries = dst_ref.shape[0]
    per_block = entries // ice
    nbl = outs[0].shape[1]
    count = list_ref[entries + UNROLL]
    groups = lax.div(count + UNROLL - 1, UNROLL)

    def compute(base, slot):
        for q in range(UNROLL):
            e = list_ref[base + q]
            s = jnp.where(base + q < count, flux[lax.div(e, per_block)], 0.0).astype(BF16)
            part = lax.dot_general(
                s, buf[slot + q], (((1,), (0,)), ((), ())), preferred_element_type=F32
            )
            at = dst_ref[e]
            for f in range(3):
                back[f, pl.ds(at, 1), :] = back[f, pl.ds(at, 1), :] + part[f : f + 1]

    start, loop = stream_weights(list_ref, groups, w_hbm, buf, sems, compute)
    start()
    back[...] = jnp.zeros_like(back)

    n_rows = groups_n * ice
    total = 2.0 * n_rows * BS

    def plane(c):
        return jnp.concatenate([x_ref[a, c] for a in range(groups_n)], axis=0)

    base = [plane(0), plane(1)]
    current = [plane(2), plane(3)]
    rate1 = plane(4) + 1.0
    half_strength = 0.5 * plane(5)
    lane = lax.broadcasted_iota(jnp.int32, (n_rows, BS), 1)
    row = lax.broadcasted_iota(jnp.int32, (n_rows, BS), 0)

    def picard(u):
        left, right = [], []
        for z in u:
            a = pltpu.roll(z, 1, 1)
            b = pltpu.roll(a, 1, 0)
            b = jnp.where(row == 0, 0.0, b)
            left.append(jnp.where(lane == 0, b, a))
            a = pltpu.roll(z, BS - 1, 1)
            b = pltpu.roll(a, n_rows - 1, 0)
            b = jnp.where(row == n_rows - 1, 0.0, b)
            right.append(jnp.where(lane == BS - 1, b, a))
        sx = 0.5 * (right[0] - left[0])
        sy = 0.5 * (right[1] - left[1])
        zeta = half_strength / jnp.sqrt(sx * sx + sy * sy + 0.25)
        den = 1.0 / (rate1 + 2.0 * zeta)
        return [(base[c] + zeta * (left[c] + right[c])) * den for c in range(2)]

    def dot(a, b):
        return jnp.sum(a[0] * b[0] + a[1] * b[1], keepdims=True) / total

    gvals, fvals, df, dg, gram, norms = [], [], [], [], {}, []
    for step in range(ITERS):
        gnew = picard(current)
        f = [gnew[c] - current[c] for c in range(2)]
        if step == 0:
            gvals, fvals = gnew, f
            current = gnew
            continue
        df.append([f[c] - fvals[c] for c in range(2)])
        dg.append([gnew[c] - gvals[c] for c in range(2)])
        gvals, fvals = gnew, f
        j = step - 1
        for i in range(j + 1):
            gram[i, j] = dot(df[i], df[j])
        norms.append(jnp.sqrt(gram[j, j] + 1e-06))
        used = list(range(max(0, step - DEPTH), step))
        m = len(used)
        a = [[None] * m for _ in range(m)]
        for p in range(m):
            for q in range(p + 1):
                i, k = used[q], used[p]
                a[p][q] = gram[i, k] / (norms[i] * norms[k])
            a[p][p] = a[p][p] + 0.1
        h = [dot(df[i], f) / norms[i] for i in used]
        d = [None] * m
        low = [[None] * m for _ in range(m)]
        y = [None] * m
        for p in range(m):
            acc = h[p]
            for q in range(p):
                v = a[p][q]
                for s in range(q):
                    v = v - low[p][s] * low[q][s] * d[s]
                low[p][q] = v / d[q]
                acc = acc - low[p][q] * y[q]
            v = a[p][p]
            for s in range(p):
                v = v - low[p][s] * low[p][s] * d[s]
            d[p] = v
            y[p] = acc
        coef = [None] * m
        for p in reversed(range(m)):
            v = y[p] / d[p]
            for q in range(p + 1, m):
                v = v - low[q][p] * coef[q]
            coef[p] = v
        current = list(gnew)
        for p, i in enumerate(used):
            scale = coef[p] / norms[i]
            for c in range(2):
                current[c] = current[c] - scale * dg[i][c]
    fin[0] = current[0]
    fin[1] = current[1]
    mine = pl.multiple_of(me_ref[0] * ice, ice)
    own = [fin[c, pl.ds(mine, ice), :] for c in range(2)]
    planes = [own[0] - rem_ref[1], own[1] - rem_ref[2], rem_ref[0]]
    for r in range(ice):
        for c in range(2):
            ice_ref[c : c + 1, r * BS : (r + 1) * BS] = own[c][r : r + 1]
        for f in range(3):
            flux[r, f : f + 1, :] = planes[f][r : r + 1]
        flux[r, 3:4, :] = jnp.zeros((1, BS), F32)
    loop()
    for k in range(groups_n):
        outs[k][...] = back[:, k * nbl : (k + 1) * nbl, :]


def solve(dst, lst, me, x, rem, weights, nbl):
    groups_n, _, ice, _ = x.shape
    chunk = jax.ShapeDtypeStruct((3, nbl, BS), F32)
    return pl.pallas_call(
        solve_kernel,
        in_specs=[SM, SM, SM, VM, VM, ANY],
        out_specs=[VM] * (groups_n + 1),
        out_shape=[chunk] * groups_n + [jax.ShapeDtypeStruct((2, ice * BS), F32)],
        scratch_shapes=[
            pltpu.VMEM((2, groups_n * ice, BS), F32),
            pltpu.VMEM((ice, 4, BS), F32),
            pltpu.VMEM((3, groups_n * nbl, BS), F32),
            pltpu.VMEM((BWD_SLOTS, BS, BS), BF16),
            pltpu.SemaphoreType.DMA((BWD_SLOTS,)),
        ],
        compiler_params=params(),
        name="solve",
    )(dst, lst, me, x, rem, weights)


def finish_kernel(*refs):
    chunks = refs[:-3]
    t_ref, flux_ref, out_ref = refs[-3:]
    height, across = t_ref.shape[2:]
    for f in range(3):
        for h in range(across // BS):
            v = chunks[0][f, h * height : (h + 1) * height, :]
            for c in chunks[1:]:
                v = v + c[f, h * height : (h + 1) * height, :]
            flux_ref[f, :, h * BS : (h + 1) * BS] = v
    out_ref[0, 0] = t_ref[0, 0] + 0.5 * flux_ref[2]


def finish(chunks, tracers_next):
    height, across = tracers_next.shape[2:]
    whole = pl.BlockSpec(chunks[0].shape, lambda i: (0, 0, 0))
    level = pl.BlockSpec((1, 1, height, across), lambda i: (0, 0, 0, 0))
    return pl.pallas_call(
        finish_kernel,
        grid=(1,),
        in_specs=[whole] * len(chunks) + [level],
        out_specs=[pl.BlockSpec((3, height, across), lambda i: (0, 0, 0)), level],
        out_shape=[
            jax.ShapeDtypeStruct((3, height, across), F32),
            jax.ShapeDtypeStruct(tracers_next.shape, F32),
        ],
        input_output_aliases={len(chunks): 1},
        name="finish",
    )(*chunks, tracers_next)


def neighbours(low_edge, high_edge, axis):
    n = lax.axis_size(axis)
    up = [(i, i + 1) for i in range(n - 1)]
    down = [(i + 1, i) for i in range(n - 1)]
    return lax.ppermute(high_edge, axis, up), lax.ppermute(low_edge, axis, down)


def coupled_step(
    tracers,
    velocity,
    remap_weights,
    remap_blocks,
    remap_count,
    ice_velocity,
    ice_mass_rate,
    ice_strength,
    wind_stress,
):
    n_grp = lax.axis_size("grp")
    n_ocn = lax.axis_size("ocn")
    column = lax.axis_index("ocn")
    me = lax.axis_index("grp")
    height, across = tracers.shape[2:]
    halves = across // BS
    nbl = height * halves
    ice, per_block = remap_blocks.shape
    weights = remap_weights.reshape(ice * per_block, BS, BS)

    local = remap_blocks % (n_grp * nbl)
    tile = local // nbl
    j = local % nbl
    place = (j % halves) * height + j // halves
    mine = (jnp.arange(per_block)[None, :] < remap_count[:, None]) & (
        remap_blocks // (n_grp * nbl) == column
    )
    code = jnp.where(mine, tile * (4 * nbl) + place, -1).reshape(-1)
    dst = (((tile - me) % n_grp) * nbl + place).reshape(-1)

    row0, rown, col0, coln = pack_edges(tracers)
    south, north = neighbours(row0, rown, "grp")
    west, east = neighbours(col0, coln, "ocn")

    surf = lax.all_gather(pack_surface(tracers, velocity), "grp", axis=0, tiled=True)
    part, lst = forward(code, surf, weights, ice)
    if n_ocn & (n_ocn - 1) == 0:
        parts = [part]
        for k in range(1, n_ocn):
            parts.append(lax.ppermute(part, "ocn", [(i, i ^ k) for i in range(n_ocn)]))
    else:
        parts = [lax.psum(part, "ocn")]
    x, rem = combine(
        parts,
        ice_velocity,
        wind_stress,
        ice_mass_rate.reshape(ice, BS),
        ice_strength.reshape(ice, BS),
    )
    xg = lax.all_gather(x, "grp", axis=0)
    *chunks, ice_final = solve(dst, lst, me.reshape(1), xg, rem, weights, nbl)
    moved = [chunks[0]]
    for k in range(1, n_grp):
        ring = [(i, (i + k) % n_grp) for i in range(n_grp)]
        moved.append(lax.ppermute(chunks[k], "grp", ring))
    tracers_next = stencil(tracers, velocity, north, south, east, west)
    surface_flux, tracers_next = finish(moved, tracers_next)
    return tracers_next, surface_flux, ice_final


def solution(mesh):
    return jax.shard_map(
        coupled_step,
        mesh=mesh,
        in_specs=(
            P(None, None, "grp", "ocn"),
            P(None, None, "grp", "ocn"),
            P("grp", None, None, None),
            P("grp", None),
            P("grp"),
            P(None, "grp"),
            P("grp"),
            P("grp"),
            P(None, "grp"),
        ),
        out_specs=(P(None, None, "grp", "ocn"), P(None, "grp", "ocn"), P(None, "grp")),
        check_vma=False,
    )
```

profile of v0, /device:TPU:0, one launch (start us, length us, event | category | flops | bytes accessed | tf_op | source)
XLA Modules:
  0.0 81.8 jit_solution(8869975968606538173)
XLA Ops:
  0.6 0.7 add_select_fusion.7
  1.5 1.5 %surface.1 = bf16[4,64,128]{2,1,0:T(8,128)(2,1)} custom-call(f32[2,32,32,256]{3,2,1,0:T(8,128)} %dn_ref.1, f32[2,32,32,256]{3,2,1,0:T(8,128)} %v_ref.3), custom_call_target="tpu_custom_call" | custom-call | tf_op jit(solution)/shard_map/surface/pallas_call | solution.py:42
  3.0 11.6 %all_gather.9.surf_ref = bf16[32,64,128]{2,1,0:T(8,128)(2,1)S(1)} all-gather(bf16[4,64,128]{2,1,0:T(8,128)(2,1)} %surface.1), channel_id=1, replica_groups=mesh['ocn'=4,'grp'=8] {'grp'}, dimensions={0}, use_global_device_ids=true | all-gather | bytes 589824 | tf_op jit(solution)/shard_map/all_gather | solution.py:511
  14.7 5.0 %forward.1 = (f32[3,32,128]{2,1,0:T(8,128)S(1)}, s32[272]{0:T(512)S(1)}) custom-call(s32[256]{0:T(256)S(1)} %reshape.26.code_ref, bf16[32,64,128]{2,1,0:T(8,128)(2,1)S(1)} %all_gather.9.surf_ref, bf16[256,128,128]{2,1,0:T(8,128)(2,1)} %bitcast.6), custom_call_target="tpu_custom_call" | custom-call | tf_op jit(solution)/shard_map/forward/pallas_call | solution.py:240
  19.6 4.3 %collective-permute-start.2 = (f32[3,32,128]{2,1,0:T(8,128)S(1)}, f32[3,32,128]{2,1,0:T(8,128)S(1)}, u32[]{:S(2)}, u32[]{:S(2)}) collective-permute-start(f32[3,32,128]{2,1,0:T(8,128)S(1)} %get-tuple-element.23.refs_0_), channel_id=1, source_target_pairs={{0,24},{8,16},{16,8},{24,0},{1,25},{9,17},{17,9},{25,1},{2,26},{10... | collective-permute-start | bytes 147464 | tf_op jit(solution)/shard_map/ppermute | solution.py:516
  24.7 1.3 %collective-permute-done.2.refs_3_ = f32[3,32,128]{2,1,0:T(8,128)S(1)} collective-permute-done((f32[3,32,128]{2,1,0:T(8,128)S(1)}, f32[3,32,128]{2,1,0:T(8,128)S(1)}, u32[]{:S(2)}, u32[]{:S(2)}) %collective-permute-start.2) | collective-permute-done | bytes 49184 | tf_op jit(solution)/shard_map/ppermute | solution.py:516
  26.0 2.9 %collective-permute-done.1.refs_2_ = f32[3,32,128]{2,1,0:T(8,128)S(1)} collective-permute-done((f32[3,32,128]{2,1,0:T(8,128)S(1)}, f32[3,32,128]{2,1,0:T(8,128)S(1)}, u32[]{:S(2)}, u32[]{:S(2)}) %collective-permute-start.1) | collective-permute-done | bytes 49184 | tf_op jit(solution)/shard_map/ppermute | solution.py:516
  29.5 1.6 %combine.1 = (f32[6,32,128]{2,1,0:T(8,128)}, f32[3,32,128]{2,1,0:T(8,128)}) custom-call(f32[3,32,128]{2,1,0:T(8,128)} %copy-done.2, f32[3,32,128]{2,1,0:T(8,128)} %copy-done.14, f32[3,32,128]{2,1,0:T(8,128)} %copy-done.13, f32[3,32,128]{2,1,0:T(8,128)} %copy-done.12, f32[2,4096]{1,0:T(2,128)} %refs_4_.1, f32[2,4096]{1,0:T(2,128)} %refs_5_.1, ...), custom_call_target="tpu_custom_call" | custom-call | tf_op jit(solution)/shard_map/combine/pallas_call | solution.py:281
  31.1 10.1 %all-gather = f32[48,32,128]{2,1,0:T(8,128)S(1)} all-gather(f32[6,32,128]{2,1,0:T(8,128)} %get-tuple-element.24), channel_id=2, replica_groups=mesh['ocn'=4,'grp'=8] {'grp'}, dimensions={0}, use_global_device_ids=true | all-gather | bytes 884736 | tf_op jit(solution)/shard_map/all_gather | solution.py:526
  41.2 0.8 copy-done.1
  42.0 5.8 %solve.1 = (f32[3,64,128]{2,1,0:T(8,128)S(1)}, f32[3,64,128]{2,1,0:T(8,128)S(1)}, f32[3,64,128]{2,1,0:T(8,128)S(1)}, f32[3,64,128]{2,1,0:T(8,128)S(1)}, f32[3,64...) custom-call(s32[256]{0:T(256)S(1)} %reshape.25.dst_ref, ...), custom_call_target="tpu_custom_call" | custom-call | tf_op jit(solution)/shard_map/solve/pallas_call | solution.py:421
  48.6 3.7 %edges.1 = (f32[2,32,256]{2,1,0:T(8,128)}, f32[2,32,256]{2,1,0:T(8,128)}, f32[32,128]{1,0:T(8,128)}, f32[32,128]{1,0:T(8,128)}) custom-call(f32[2,32,32,256]{3,2,1,0:T(8,128)} %dn_ref.1), custom_call_target="tpu_custom_call" | custom-call | tf_op jit(solution)/shard_map/edges/pallas_call | solution.py:85
  52.3 1.3 %collective-permute-start.10 = (f32[2,32,256]{2,1,0:T(8,128)}, f32[2,32,256]{2,1,0:T(8,128)S(1)}, u32[]{:S(2)}, u32[]{:S(2)}) collective-permute-start(f32[2,32,256]{2,1,0:T(8,128)} %get-tuple-element.34), channel_id=1, source_target_pairs={{1,0},{2,1},{3,2},{4,3},{5,4},{6,5},{7,6},{9,8},{10,9},{11,10},{12... | collective-permute-start | bytes 196616 | tf_op jit(solution)/shard_map/ppermute | solution.py:473
  53.6 3.5 %collective-permute-start.11 = (f32[2,32,256]{2,1,0:T(8,128)}, f32[2,32,256]{2,1,0:T(8,128)S(1)}, u32[]{:S(2)}, u32[]{:S(2)}) collective-permute-start(f32[2,32,256]{2,1,0:T(8,128)} %get-tuple-element.35), channel_id=1, source_target_pairs={{0,1},{1,2},{2,3},{3,4},{4,5},{5,6},{6,7},{8,9},{9,10},{10,11},{11... | collective-permute-start | bytes 196616 | tf_op jit(solution)/shard_map/ppermute | solution.py:473
  57.1 1.3 %collective-permute-start.12 = (f32[32,128]{1,0:T(8,128)}, f32[32,128]{1,0:T(8,128)S(1)}, u32[]{:S(2)}, u32[]{:S(2)}) collective-permute-start(f32[32,128]{1,0:T(8,128)} %get-tuple-element.36), channel_id=1, source_target_pairs={{8,0},{16,8},{24,16},{9,1},{17,9},{25,17},{10,2},{18,10},{26,18},{... | collective-permute-start | bytes 49160 | tf_op jit(solution)/shard_map/ppermute | solution.py:473
  58.4 4.5 %collective-permute-done.12.east_ref = f32[32,128]{1,0:T(8,128)S(1)} collective-permute-done((f32[32,128]{1,0:T(8,128)}, f32[32,128]{1,0:T(8,128)S(1)}, u32[]{:S(2)}, u32[]{:S(2)}) %collective-permute-start.12) | collective-permute-done | bytes 16416 | tf_op jit(solution)/shard_map/ppermute | solution.py:473
  63.0 2.5 %collective-permute-start.13 = (f32[32,128]{1,0:T(8,128)}, f32[32,128]{1,0:T(8,128)S(1)}, u32[]{:S(2)}, u32[]{:S(2)}) collective-permute-start(f32[32,128]{1,0:T(8,128)} %get-tuple-element.37), channel_id=1, source_target_pairs={{0,8},{8,16},{16,24},{1,9},{9,17},{17,25},{2,10},{10,18},{18,26},{... | collective-permute-start | bytes 49160 | tf_op jit(solution)/shard_map/ppermute | solution.py:473
  65.4 1.6 %collective-permute-done.13.west_ref = f32[32,128]{1,0:T(8,128)S(1)} collective-permute-done((f32[32,128]{1,0:T(8,128)}, f32[32,128]{1,0:T(8,128)S(1)}, u32[]{:S(2)}, u32[]{:S(2)}) %collective-permute-start.13) | collective-permute-done | bytes 16416 | tf_op jit(solution)/shard_map/ppermute | solution.py:473
  67.1 1.9 %collective-permute-start.5 = (f32[3,64,128]{2,1,0:T(8,128)S(1)}, f32[3,64,128]{2,1,0:T(8,128)S(1)}, u32[]{:S(2)}, u32[]{:S(2)}) collective-permute-start(f32[3,64,128]{2,1,0:T(8,128)S(1)} %get-tuple-element.29), channel_id=1, source_target_pairs={{0,3},{1,4},{2,5},{3,6},{4,7},{5,0},{6,1},{7,2},{8,11},{9,12},{10,... | collective-permute-start | bytes 294920 | tf_op jit(solution)/shard_map/ppermute | solution.py:531
  69.6 1.4 %collective-permute-start.7 = (f32[3,64,128]{2,1,0:T(8,128)S(1)}, f32[3,64,128]{2,1,0:T(8,128)S(1)}, u32[]{:S(2)}, u32[]{:S(2)}) collective-permute-start(f32[3,64,128]{2,1,0:T(8,128)S(1)} %get-tuple-element.31), channel_id=1, source_target_pairs={{0,5},{1,6},{2,7},{3,0},{4,1},{5,2},{6,3},{7,4},{8,13},{9,14},{10,... | collective-permute-start | bytes 294920 | tf_op jit(solution)/shard_map/ppermute | solution.py:531
  71.0 1.3 %collective-permute-start.8 = (f32[3,64,128]{2,1,0:T(8,128)S(1)}, f32[3,64,128]{2,1,0:T(8,128)S(1)}, u32[]{:S(2)}, u32[]{:S(2)}) collective-permute-start(f32[3,64,128]{2,1,0:T(8,128)S(1)} %get-tuple-element.32), channel_id=1, source_target_pairs={{0,6},{1,7},{2,0},{3,1},{4,2},{5,3},{6,4},{7,5},{8,14},{9,15},{10,... | collective-permute-start | bytes 294920 | tf_op jit(solution)/shard_map/ppermute | solution.py:531
  72.4 1.2 %collective-permute-start.9 = (f32[3,64,128]{2,1,0:T(8,128)S(1)}, f32[3,64,128]{2,1,0:T(8,128)S(1)}, u32[]{:S(2)}, u32[]{:S(2)}) collective-permute-start(f32[3,64,128]{2,1,0:T(8,128)S(1)} %get-tuple-element.33), channel_id=1, source_target_pairs={{0,7},{1,0},{2,1},{3,2},{4,3},{5,4},{6,5},{7,6},{8,15},{9,8},{10,9... | collective-permute-start | bytes 294920 | tf_op jit(solution)/shard_map/ppermute | solution.py:531
  73.6 5.5 %stencil.1.refs_8_ = f32[2,32,32,256]{3,2,1,0:T(8,128)} custom-call(f32[2,32,32,256]{3,2,1,0:T(8,128)} %dn_ref.1, f32[2,32,32,256]{3,2,1,0:T(8,128)} %dn_ref.1, f32[2,32,32,256]{3,2,1,0:T(8,128)} %dn_ref.1, f32[2,32,32,256]{3,2,1,0:T(8,128)} %v_ref.3, f32[2,32,256]{2,1,0:T(8,128)} %copy-done.10, f32[2,32,256]{2,1,0:T(8,128)} %copy-done.11, ...), custom_call_target="tpu_custom_call" | custom-call | flops 120000000 | bytes 8388608 | tf_op jit(solution)/shard_map/stencil/pallas_call | solution.py:140
  79.9 1.9 %finish.1 = (f32[3,32,256]{2,1,0:T(8,128)}, f32[2,32,32,256]{3,2,1,0:T(8,128)}) custom-call(f32[3,64,128]{2,1,0:T(8,128)} %copy-done, f32[3,64,128]{2,1,0:T(8,128)} %copy-done.3, f32[3,64,128]{2,1,0:T(8,128)} %copy-done.4, f32[3,64,128]{2,1,0:T(8,128)} %copy-done.5, f32[3,64,128]{2,1,0:T(8,128)} %copy-done.6, ...), custom_call_target="tpu_custom_call", output_to_operand_aliasing={{1}: (8, {})} | custom-call | tf_op jit(solution)/shard_map/finish/pallas_call | solution.py:455
  (52 shorter events, 3.8 us)
Async XLA Ops:
  19.6 9.3 %copy-start.2 = (f32[3,32,128]{2,1,0:T(8,128)}, f32[3,32,128]{2,1,0:T(8,128)S(1)}, u32[]{:S(2)}) copy-start(f32[3,32,128]{2,1,0:T(8,128)S(1)} %get-tuple-element.23.refs_0_) | copy-start | bytes 147460
  19.6 6.3 %collective-permute-start.2 = (f32[3,32,128]{2,1,0:T(8,128)S(1)}, f32[3,32,128]{2,1,0:T(8,128)S(1)}, u32[]{:S(2)}, u32[]{:S(2)}) collective-permute-start(f32[3,32,128]{2,1,0:T(8,128)S(1)} %get-tuple-element.23.refs_0_), channel_id=1, source_target_pairs={{0,24},{8,16},{16,8},{24,0},{1,25},{9,17},{17,9},{25,1},{2,26},{10... | collective-permute-start | bytes 147464 | tf_op jit(solution)/shard_map/ppermute | solution.py:516
  23.9 5.0 %collective-permute-start.1 = (f32[3,32,128]{2,1,0:T(8,128)S(1)}, f32[3,32,128]{2,1,0:T(8,128)S(1)}, u32[]{:S(2)}, u32[]{:S(2)}) collective-permute-start(f32[3,32,128]{2,1,0:T(8,128)S(1)} %get-tuple-element.23.refs_0_), channel_id=1, source_target_pairs={{0,16},{8,24},{16,0},{24,8},{1,17},{9,25},{17,1},{25,9},{2,18},{10... | collective-permute-start | bytes 147464 | tf_op jit(solution)/shard_map/ppermute | solution.py:516
  23.9 5.0 %collective-permute-start = (f32[3,32,128]{2,1,0:T(8,128)S(1)}, f32[3,32,128]{2,1,0:T(8,128)S(1)}, u32[]{:S(2)}, u32[]{:S(2)}) collective-permute-start(f32[3,32,128]{2,1,0:T(8,128)S(1)} %get-tuple-element.23.refs_0_), channel_id=1, source_target_pairs={{0,8},{8,0},{16,24},{24,16},{1,9},{9,1},{17,25},{25,17},{2,10},{10... | collective-permute-start | bytes 147464 | tf_op jit(solution)/shard_map/ppermute | solution.py:516
  26.0 2.9 %copy-start.12 = (f32[3,32,128]{2,1,0:T(8,128)}, f32[3,32,128]{2,1,0:T(8,128)S(1)}, u32[]{:S(2)}) copy-start(f32[3,32,128]{2,1,0:T(8,128)S(1)} %collective-permute-done.2.refs_3_) | copy-start | bytes 147460
  41.2 0.8 copy-start.1
  48.5 22.6 %collective-permute-start.3 = (f32[3,64,128]{2,1,0:T(8,128)S(1)}, f32[3,64,128]{2,1,0:T(8,128)S(1)}, u32[]{:S(2)}, u32[]{:S(2)}) collective-permute-start(f32[3,64,128]{2,1,0:T(8,128)S(1)} %get-tuple-element.27), channel_id=1, source_target_pairs={{0,1},{1,2},{2,3},{3,4},{4,5},{5,6},{6,7},{7,0},{8,9},{9,10},{10,1... | collective-permute-start | bytes 294920 | tf_op jit(solution)/shard_map/ppermute | solution.py:531
  48.5 23.9 %collective-permute-start.4 = (f32[3,64,128]{2,1,0:T(8,128)S(1)}, f32[3,64,128]{2,1,0:T(8,128)S(1)}, u32[]{:S(2)}, u32[]{:S(2)}) collective-permute-start(f32[3,64,128]{2,1,0:T(8,128)S(1)} %get-tuple-element.28), channel_id=1, source_target_pairs={{0,2},{1,3},{2,4},{3,5},{4,6},{5,7},{6,0},{7,1},{8,10},{9,11},{10,... | collective-permute-start | bytes 294920 | tf_op jit(solution)/shard_map/ppermute | solution.py:531
  52.3 16.7 %collective-permute-start.10 = (f32[2,32,256]{2,1,0:T(8,128)}, f32[2,32,256]{2,1,0:T(8,128)S(1)}, u32[]{:S(2)}, u32[]{:S(2)}) collective-permute-start(f32[2,32,256]{2,1,0:T(8,128)} %get-tuple-element.34), channel_id=1, source_target_pairs={{1,0},{2,1},{3,2},{4,3},{5,4},{6,5},{7,6},{9,8},{10,9},{11,10},{12... | collective-permute-start | bytes 196616 | tf_op jit(solution)/shard_map/ppermute | solution.py:473
  53.6 16.0 %collective-permute-start.11 = (f32[2,32,256]{2,1,0:T(8,128)}, f32[2,32,256]{2,1,0:T(8,128)S(1)}, u32[]{:S(2)}, u32[]{:S(2)}) collective-permute-start(f32[2,32,256]{2,1,0:T(8,128)} %get-tuple-element.35), channel_id=1, source_target_pairs={{0,1},{1,2},{2,3},{3,4},{4,5},{5,6},{6,7},{8,9},{9,10},{10,11},{11... | collective-permute-start | bytes 196616 | tf_op jit(solution)/shard_map/ppermute | solution.py:473
  57.1 5.8 %collective-permute-start.12 = (f32[32,128]{1,0:T(8,128)}, f32[32,128]{1,0:T(8,128)S(1)}, u32[]{:S(2)}, u32[]{:S(2)}) collective-permute-start(f32[32,128]{1,0:T(8,128)} %get-tuple-element.36), channel_id=1, source_target_pairs={{8,0},{16,8},{24,16},{9,1},{17,9},{25,17},{10,2},{18,10},{26,18},{... | collective-permute-start | bytes 49160 | tf_op jit(solution)/shard_map/ppermute | solution.py:473
  63.0 10.6 %copy-start.15 = (f32[32,128]{1,0:T(8,128)}, f32[32,128]{1,0:T(8,128)S(1)}, u32[]{:S(2)}) copy-start(f32[32,128]{1,0:T(8,128)S(1)} %collective-permute-done.12.east_ref) | copy-start | bytes 49156
  63.0 4.1 %collective-permute-start.13 = (f32[32,128]{1,0:T(8,128)}, f32[32,128]{1,0:T(8,128)S(1)}, u32[]{:S(2)}, u32[]{:S(2)}) collective-permute-start(f32[32,128]{1,0:T(8,128)} %get-tuple-element.37), channel_id=1, source_target_pairs={{0,8},{8,16},{16,24},{1,9},{9,17},{17,25},{2,10},{10,18},{18,26},{... | collective-permute-start | bytes 49160 | tf_op jit(solution)/shard_map/ppermute | solution.py:473
  67.1 6.5 %copy-start.16 = (f32[32,128]{1,0:T(8,128)}, f32[32,128]{1,0:T(8,128)S(1)}, u32[]{:S(2)}) copy-start(f32[32,128]{1,0:T(8,128)S(1)} %collective-permute-done.13.west_ref) | copy-start | bytes 49156
  67.1 12.0 %collective-permute-start.5 = (f32[3,64,128]{2,1,0:T(8,128)S(1)}, f32[3,64,128]{2,1,0:T(8,128)S(1)}, u32[]{:S(2)}, u32[]{:S(2)}) collective-permute-start(f32[3,64,128]{2,1,0:T(8,128)S(1)} %get-tuple-element.29), channel_id=1, source_target_pairs={{0,3},{1,4},{2,5},{3,6},{4,7},{5,0},{6,1},{7,2},{8,11},{9,12},{10,... | collective-permute-start | bytes 294920 | tf_op jit(solution)/shard_map/ppermute | solution.py:531
  69.0 4.6 %copy-start.10 = (f32[2,32,256]{2,1,0:T(8,128)}, f32[2,32,256]{2,1,0:T(8,128)S(1)}, u32[]{:S(2)}) copy-start(f32[2,32,256]{2,1,0:T(8,128)S(1)} %collective-permute-done.10.north_ref) | copy-start | bytes 196612
  69.0 10.1 %collective-permute-start.6 = (f32[3,64,128]{2,1,0:T(8,128)S(1)}, f32[3,64,128]{2,1,0:T(8,128)S(1)}, u32[]{:S(2)}, u32[]{:S(2)}) collective-permute-start(f32[3,64,128]{2,1,0:T(8,128)S(1)} %get-tuple-element.30), channel_id=1, source_target_pairs={{0,4},{1,5},{2,6},{3,7},{4,0},{5,1},{6,2},{7,3},{8,12},{9,13},{10,... | collective-permute-start | bytes 294920 | tf_op jit(solution)/shard_map/ppermute | solution.py:531
  69.6 4.0 %copy-start.11 = (f32[2,32,256]{2,1,0:T(8,128)}, f32[2,32,256]{2,1,0:T(8,128)S(1)}, u32[]{:S(2)}) copy-start(f32[2,32,256]{2,1,0:T(8,128)S(1)} %collective-permute-done.11.south_ref) | copy-start | bytes 196612
  69.6 9.5 %collective-permute-start.7 = (f32[3,64,128]{2,1,0:T(8,128)S(1)}, f32[3,64,128]{2,1,0:T(8,128)S(1)}, u32[]{:S(2)}, u32[]{:S(2)}) collective-permute-start(f32[3,64,128]{2,1,0:T(8,128)S(1)} %get-tuple-element.31), channel_id=1, source_target_pairs={{0,5},{1,6},{2,7},{3,0},{4,1},{5,2},{6,3},{7,4},{8,13},{9,14},{10,... | collective-permute-start | bytes 294920 | tf_op jit(solution)/shard_map/ppermute | solution.py:531
  71.0 8.0 %copy-start.3 = (f32[3,64,128]{2,1,0:T(8,128)}, f32[3,64,128]{2,1,0:T(8,128)S(1)}, u32[]{:S(2)}) copy-start(f32[3,64,128]{2,1,0:T(8,128)S(1)} %collective-permute-done.3.refs_1_) | copy-start | bytes 294916
  71.0 8.1 %collective-permute-start.8 = (f32[3,64,128]{2,1,0:T(8,128)S(1)}, f32[3,64,128]{2,1,0:T(8,128)S(1)}, u32[]{:S(2)}, u32[]{:S(2)}) collective-permute-start(f32[3,64,128]{2,1,0:T(8,128)S(1)} %get-tuple-element.32), channel_id=1, source_target_pairs={{0,6},{1,7},{2,0},{3,1},{4,2},{5,3},{6,4},{7,5},{8,14},{9,15},{10,... | collective-permute-start | bytes 294920 | tf_op jit(solution)/shard_map/ppermute | solution.py:531
  72.4 6.7 %copy-start.4 = (f32[3,64,128]{2,1,0:T(8,128)}, f32[3,64,128]{2,1,0:T(8,128)S(1)}, u32[]{:S(2)}) copy-start(f32[3,64,128]{2,1,0:T(8,128)S(1)} %collective-permute-done.4.refs_2_) | copy-start | bytes 294916
  72.4 6.8 %collective-permute-start.9 = (f32[3,64,128]{2,1,0:T(8,128)S(1)}, f32[3,64,128]{2,1,0:T(8,128)S(1)}, u32[]{:S(2)}, u32[]{:S(2)}) collective-permute-start(f32[3,64,128]{2,1,0:T(8,128)S(1)} %get-tuple-element.33), channel_id=1, source_target_pairs={{0,7},{1,0},{2,1},{3,2},{4,3},{5,4},{6,5},{7,6},{8,15},{9,8},{10,9... | collective-permute-start | bytes 294920 | tf_op jit(solution)/shard_map/ppermute | solution.py:531
  79.1 0.7 copy-start.8
  (7 other events, 4.5 us)
where the time goes:
time: 82.8 us; the launch traced here: 81.8 us
  Pallas kernels  24.9 us (30%)
  blocking collectives  21.7 us (26%)
  starting transfers between devices  20.1 us (24%)
  waiting for transfers between devices  10.4 us (13%)
  local copies, waits for them, and re-layouts  3.1 us (4%)
  between operations  0.83 us (1%)
    all_gather x1, blocking collectives, coupled_step(): lax.all_gather(pack_surface(tracers, velocity), 'grp', axis=0, tiled=True)  11.6 us
    all_gather x1, blocking collectives, coupled_step(): xg = lax.all_gather(x, 'grp', axis=0)  10.1 us
    ppermute x7, starting transfers between devices, coupled_step(): moved.append(lax.ppermute(chunks[k], 'grp', ring))  6.66 us
    ppermute x2, starting transfers between devices, neighbours(): lax.ppermute(high_edge, axis, up)  5.93 us
    pallas_call x1, Pallas kernels, solve(): pl.pallas_call(solve_kernel, in_specs=[SM, SM, SM, VM, VM, ANY], out_spec...  5.8 us
    pallas_call x1, Pallas kernels, stencil(): pl.pallas_call(stencil_kernel, grid=(levels // lc,), in_specs=[main, up,...  5.47 us
    pallas_call x1, Pallas kernels, forward(): pl.pallas_call(forward_kernel, in_specs=[SM, VM, ANY], out_specs=[VM, SM]...  4.96 us
    ppermute x3, starting transfers between devices, coupled_step(): parts.append(lax.ppermute(part, 'ocn', [(i, i ^ k) for i in range(n_ocn)]))  4.92 us
  transfers between devices with their start and end apart: 14, of which 4 were waited for; matrix products, arithmetic and copies ran while one was open for 0% of the time, Pallas kernels for 11%

commit v1 on v0

--- a/solution.py
+++ b/solution.py
@@ -1,3 +1,5 @@
+import functools
+
 import jax
 import jax.numpy as jnp
 from jax import lax
@@ -18,90 +20,90 @@
 
 VM = pl.BlockSpec(memory_space=pltpu.VMEM)
 SM = pl.BlockSpec(memory_space=pltpu.SMEM)
-ANY = pl.BlockSpec(memory_space=pl.ANY)
-
-
-def params(**kw):
-    return pltpu.CompilerParams(vmem_limit_bytes=48 * 1024 * 1024, **kw)
-
-
-def surface_kernel(t_ref, v_ref, out_ref):
-    height, across = t_ref.shape[2], t_ref.shape[3]
+ANY = pl.BlockSpec(memory_space=pltpu.HBM)
+
+
+def in_hbm(x):
+    return pltpu.with_memory_space_constraint(x, pltpu.HBM)
+
+
+def params(mib):
+    return pltpu.CompilerParams(vmem_limit_bytes=mib * 1024 * 1024)
+
+
+def surface_kernel(code_ref, t_hbm, v_hbm, out_ref, list_ref, buf, sems):
+    height, across = buf.shape[1:]
+    entries = code_ref.shape[0]
+    copies = [
+        pltpu.make_async_copy(
+            (t_hbm if f < 2 else v_hbm).at[f % 2, 0], buf.at[f], sems.at[f]
+        )
+        for f in range(4)
+    ]
+    for c in copies:
+        c.start()
+
+    def scan(i, n):
+        for q in range(8):
+            e = i * 8 + q
+            list_ref[n] = e
+            n = n + jnp.where(code_ref[e] >= 0, 1, 0)
+        return n
+
+    count = lax.fori_loop(0, entries // 8, scan, 0)
+    for q in range(UNROLL):
+        list_ref[count + q] = 0
+    list_ref[entries + UNROLL] = count
+    for c in copies:
+        c.wait()
     for f in range(4):
-        src = t_ref if f < 2 else v_ref
         for h in range(across // BS):
-            out_ref[f, h * height : (h + 1) * height, :] = src[
-                f % 2, 0, :, h * BS : (h + 1) * BS
+            out_ref[f, h * height : (h + 1) * height, :] = buf[
+                f, :, h * BS : (h + 1) * BS
             ].astype(BF16)
 
 
-def pack_surface(tracers, velocity):
+def pack_surface(code, tracers, velocity):
     height, across = tracers.shape[2:]
-    spec = pl.BlockSpec((2, 1, height, across), lambda i: (0, 0, 0, 0))
     nbl = height * across // BS
     return pl.pallas_call(
         surface_kernel,
-        grid=(1,),
-        in_specs=[spec, spec],
-        out_specs=pl.BlockSpec((4, nbl, BS), lambda i: (0, 0, 0)),
-        out_shape=jax.ShapeDtypeStruct((4, nbl, BS), BF16),
+        in_specs=[SM, ANY, ANY],
+        out_specs=[VM, SM],
+        out_shape=[
+            jax.ShapeDtypeStruct((4, nbl, BS), BF16),
+            jax.ShapeDtypeStruct((code.shape[0] + UNROLL + 8,), jnp.int32),
+        ],
+        scratch_shapes=[
+            pltpu.VMEM((4, height, across), F32),
+            pltpu.SemaphoreType.DMA((4,)),
+        ],
+        compiler_params=params(4),
         name="surface",
-    )(tracers, velocity)
-
-
-def edges_kernel(t_ref, row0_ref, rown_ref, col0_ref, coln_ref):
-    step = pl.program_id(0)
-    lc, height, across = t_ref.shape[1:]
-    levels = lc * pl.num_programs(0)
-    lane = lax.broadcasted_iota(jnp.int32, (height, BS), 1)
-
-    @pl.when(step == 0)
-    def _():
-        col0_ref[...] = jnp.zeros_like(col0_ref)
-        coln_ref[...] = jnp.zeros_like(coln_ref)
-
-    first = col0_ref[...]
-    last = coln_ref[...]
-    for t in range(2):
-        for i in range(lc):
-            c = t * levels + step * lc + i
-            first = jnp.where(lane == c, pltpu.roll(t_ref[t, i, :, :BS], c, 1), first)
-            last = jnp.where(
-                lane == c, pltpu.roll(t_ref[t, i, :, across - BS :], (c + 1) % BS, 1), last
-            )
-            row0_ref[t, i : i + 1, :] = t_ref[t, i, 0:1, :]
-            rown_ref[t, i : i + 1, :] = t_ref[t, i, height - 1 : height, :]
-    col0_ref[...] = first
-    coln_ref[...] = last
-
-
-def pack_edges(tracers):
-    _, levels, height, across = tracers.shape
-    lc = 8
-    rows = jax.ShapeDtypeStruct((2, levels, across), F32)
-    cols = jax.ShapeDtypeStruct((height, BS), F32)
-    row_spec = pl.BlockSpec((2, lc, across), lambda i: (0, i, 0))
-    col_spec = pl.BlockSpec((height, BS), lambda i: (0, 0))
-    return pl.pallas_call(
-        edges_kernel,
-        grid=(levels // lc,),
-        in_specs=[pl.BlockSpec((2, lc, height, across), lambda i: (0, i, 0, 0))],
-        out_specs=[row_spec, row_spec, col_spec, col_spec],
-        out_shape=[rows, rows, cols, cols],
-        name="edges",
-    )(tracers)
-
-
-def stencil_kernel(t_ref, up_ref, dn_ref, v_ref, north_ref, south_ref, east_ref, west_ref, out_ref):
+    )(code, in_hbm(tracers), in_hbm(velocity))
+
+
+def stencil_kernel(
+    n_grp, me_ref, t_ref, up_ref, dn_ref, v_ref, south_ref, north_ref, cols_ref, out_ref
+):
     step = pl.program_id(0)
     steps = pl.num_programs(0)
     lc, height, across = t_ref.shape[1:]
+    halves = across // BS
     levels = lc * steps
+    skip = south_ref.shape[0] - 2 * levels * halves
     lane = lax.broadcasted_iota(jnp.int32, (height, across), 1)
     row = lax.broadcasted_iota(jnp.int32, (height, across), 0)
     pad = jnp.zeros((height, across - BS), F32)
     top = jnp.where(step == 0, 0.0, 1.0)
     bottom = jnp.where(step == steps - 1, 0.0, 1.0)
+    no_south = jnp.where(me_ref[0] == 0, 0.0, 1.0)
+    no_north = jnp.where(me_ref[0] == n_grp - 1, 0.0, 1.0)
+
+    def outer_row(ref, c):
+        pieces = [ref[pl.ds(skip + h * 2 * levels + c, 1), :] for h in range(halves)]
+        return jnp.concatenate(pieces, axis=1)
+
     for i in range(lc):
         u = v_ref[0, i]
         v = v_ref[1, i]
@@ -110,14 +112,15 @@
             x = t_ref[t, i]
             above = up_ref[t, 0] * top if i == 0 else t_ref[t, i - 1]
             below = dn_ref[t, 0] * bottom if i == lc - 1 else t_ref[t, i + 1]
-            wcol = jnp.concatenate(
-                [pltpu.roll(west_ref[...], (BS - c) % BS, 1), pad], axis=1
-            )
-            ecol = jnp.concatenate([pad, pltpu.roll(east_ref[...], BS - 1 - c, 1)], axis=1)
+            cols = cols_ref[...]
+            wcol = jnp.concatenate([pltpu.roll(cols, BS // 2 - c, 1), pad], axis=1)
+            ecol = jnp.concatenate([pad, pltpu.roll(cols, BS - 1 - c, 1)], axis=1)
+            south = outer_row(south_ref, c) * no_south
+            north = outer_row(north_ref, c) * no_north
             w = jnp.where(lane == 0, wcol, pltpu.roll(x, 1, 1))
             e = jnp.where(lane == across - 1, ecol, pltpu.roll(x, across - 1, 1))
-            s = jnp.where(row == 0, south_ref[t, i : i + 1, :], pltpu.roll(x, 1, 0))
-            n = jnp.where(row == height - 1, north_ref[t, i : i + 1, :], pltpu.roll(x, height - 1, 0))
+            s = jnp.where(row == 0, south, pltpu.roll(x, 1, 0))
+            n = jnp.where(row == height - 1, north, pltpu.roll(x, height - 1, 0))
             advect = u * (e - w) * 0.5 + v * (n - s) * 0.5
             out_ref[t, i] = (
                 x
@@ -127,7 +130,7 @@
             )
 
 
-def stencil(tracers, velocity, north, south, east, west):
+def stencil(me, n_grp, tracers, velocity, south, north, cols):
     _, levels, height, across = tracers.shape
     lc = 8
     main = pl.BlockSpec((2, lc, height, across), lambda i: (0, i, 0, 0))
@@ -135,19 +138,18 @@
     dn = pl.BlockSpec(
         (2, 1, height, across), lambda i: (0, jnp.minimum(i * lc + lc, levels - 1), 0, 0)
     )
-    row_spec = pl.BlockSpec((2, lc, across), lambda i: (0, i, 0))
-    col_spec = pl.BlockSpec((height, BS), lambda i: (0, 0))
-    return pl.pallas_call(
-        stencil_kernel,
+    return pl.pallas_call(
+        functools.partial(stencil_kernel, n_grp),
         grid=(levels // lc,),
-        in_specs=[main, up, dn, main, row_spec, row_spec, col_spec, col_spec],
+        in_specs=[SM, main, up, dn, main, VM, VM, VM],
         out_specs=main,
         out_shape=jax.ShapeDtypeStruct(tracers.shape, F32),
+        compiler_params=params(14),
         cost_estimate=pl.CostEstimate(
             flops=120_000_000, bytes_accessed=4 * tracers.size * 4, transcendentals=0
         ),
         name="stencil",
-    )(tracers, tracers, tracers, velocity, north, south, east, west)
+    )(me, tracers, tracers, tracers, velocity, south, north, cols)
 
 
 def stream_weights(list_ref, groups, w_hbm, buf, sems, compute):
@@ -184,23 +186,14 @@
     return start, loop
 
 
-def forward_kernel(code_ref, surf_ref, w_hbm, out_ref, list_ref, rows, acc, buf, sems):
+def forward_kernel(
+    code_ref, list_ref, surf_ref, w_hbm, t_hbm, out_ref, row0_ref, rown_ref, rows, acc, tiles, buf, sems, t_sem
+):
     entries = code_ref.shape[0]
     ice = acc.shape[0]
     per_block = entries // ice
     nbl = surf_ref.shape[1]
-
-    def scan(i, n):
-        for q in range(8):
-            e = i * 8 + q
-            list_ref[n] = e
-            n = n + jnp.where(code_ref[e] >= 0, 1, 0)
-        return n
-
-    count = lax.fori_loop(0, entries // 8, scan, 0)
-    for q in range(UNROLL):
-        list_ref[count + q] = 0
-    list_ref[entries + UNROLL] = count
+    count = list_ref[entries + UNROLL]
     groups = lax.div(count + UNROLL - 1, UNROLL)
     first = lax.broadcasted_iota(jnp.int32, (4, BS), 0)
 
@@ -222,6 +215,8 @@
 
     start, loop = stream_weights(list_ref, groups, w_hbm, buf, sems, compute)
     start()
+    whole = pltpu.make_async_copy(t_hbm, tiles, t_sem)
+    whole.start()
     planes = surf_ref.shape[0]
     for p in range(planes):
         rows[p * nbl : (p + 1) * nbl, :] = surf_ref[p].astype(F32)
@@ -233,70 +228,115 @@
         out_ref[1, r : r + 1, :] = a[2:3]
         out_ref[2, r : r + 1, :] = a[3:4]
 
-
-def forward(code, surf, weights, ice):
-    entries = weights.shape[0]
+    _, levels, height, across = tiles.shape
+    whole.wait()
+    lane = lax.broadcasted_iota(jnp.int32, (height, BS), 1)
+    cols = jnp.zeros((height, BS), F32)
+    for t in range(2):
+        for i in range(levels):
+            c = t * levels + i
+            low = pltpu.roll(tiles[t, i, :, :BS], c, 1)
+            high = pltpu.roll(tiles[t, i, :, across - BS :], (BS // 2 + c + 1) % BS, 1)
+            cols = jnp.where(lane == c, low, jnp.where(lane == BS // 2 + c, high, cols))
+            for h in range(across // BS):
+                at = h * 2 * levels + c
+                row0_ref[at : at + 1, :] = tiles[t, i, 0:1, h * BS : (h + 1) * BS]
+                rown_ref[at : at + 1, :] = tiles[t, i, height - 1 : height, h * BS : (h + 1) * BS]
+    out_ref[3] = cols
+
+
+def forward(code, lst, surf, weights, tracers, ice):
     planes, nbl = surf.shape[:2]
+    _, levels, height, across = tracers.shape
+    assert 4 * levels == BS and height == ice
+    edge = jax.ShapeDtypeStruct((2 * levels * (across // BS), BS), F32)
     return pl.pallas_call(
         forward_kernel,
-        in_specs=[SM, VM, ANY],
-        out_specs=[VM, SM],
-        out_shape=[
-            jax.ShapeDtypeStruct((3, ice, BS), F32),
-            jax.ShapeDtypeStruct((entries + UNROLL + 8,), jnp.int32),
-        ],
+        in_specs=[SM, SM, VM, ANY, ANY],
+        out_specs=[VM, VM, VM],
+        out_shape=[jax.ShapeDtypeStruct((4, ice, BS), F32), edge, edge],
         scratch_shapes=[
             pltpu.VMEM((planes * nbl, BS), F32),
             pltpu.VMEM((ice, 4, BS), F32),
+            pltpu.VMEM(tracers.shape, F32),
             pltpu.VMEM((FWD_SLOTS, BS, BS), BF16),
             pltpu.SemaphoreType.DMA((FWD_SLOTS,)),
+            pltpu.SemaphoreType.DMA(()),
         ],
-        compiler_params=params(),
+        compiler_params=params(12),
         name="forward",
-    )(code, surf, weights)
-
-
-def combine_kernel(*refs):
-    parts = refs[:-6]
-    u_ref, wind_ref, rate_ref, strength_ref, x_ref, rem_ref = refs[-6:]
-    vals = [p[...] for p in parts]
+    )(code, lst, surf, in_hbm(weights), in_hbm(tracers))
+
+
+def icerows_kernel(u_ref, wind_ref, rate_ref, strength_ref, x_ref):
+    ice = rate_ref.shape[0]
+    for r in range(ice):
+        for c in range(2):
+            x_ref[2 + c, r : r + 1, :] = u_ref[c : c + 1, r * BS : (r + 1) * BS]
+            x_ref[c, r : r + 1, :] = wind_ref[c : c + 1, r * BS : (r + 1) * BS]
+    rate = rate_ref[...]
+    for c in range(2):
+        x_ref[c] = rate * x_ref[2 + c] + x_ref[c]
+    x_ref[4] = rate
+    x_ref[5] = strength_ref[...]
+
+
+def ice_rows(u, wind, rate, strength):
+    return pl.pallas_call(
+        icerows_kernel,
+        in_specs=[VM] * 4,
+        out_specs=VM,
+        out_shape=jax.ShapeDtypeStruct((6,) + rate.shape, F32),
+        compiler_params=params(2),
+        name="icerows",
+    )(u, wind, rate, strength)
+
+
+def combine_kernel(ocn_ref, *refs):
+    parts = refs[:-4]
+    rows_ref, x_ref, rem_ref, cols_ref = refs[-4:]
+    me, n = ocn_ref[0], len(parts)
+    vals = [p[0:3] for p in parts]
     while len(vals) > 1:
         vals = [a + b for a, b in zip(vals[0::2], vals[1::2])]
     rem_ref[...] = vals[0]
-    ice = rate_ref.shape[0]
-    for r in range(ice):
-        for c in range(2):
-            u = u_ref[c : c + 1, r * BS : (r + 1) * BS]
-            x_ref[2 + c, r : r + 1, :] = u
-            x_ref[c, r : r + 1, :] = wind_ref[c : c + 1, r * BS : (r + 1) * BS]
-    rate = rate_ref[...]
+    x_ref[...] = rows_ref[...]
     for c in range(2):
-        x_ref[c] = rate * x_ref[2 + c] + x_ref[c] + rem_ref[1 + c]
-    x_ref[4] = rate
-    x_ref[5] = strength_ref[...]
-
-
-def combine(parts, u, wind, rate, strength):
-    ice = rate.shape[0]
+        x_ref[c] = rows_ref[c] + vals[0][1 + c]
+    to_east = jnp.where(me < n - 1, me ^ (me + 1), 0)
+    to_west = jnp.where(me > 0, me ^ (me - 1), 0)
+    east = jnp.zeros(cols_ref.shape, F32)
+    west = east
+    for k in range(1, n):
+        east = jnp.where(to_east == k, parts[k][3], east)
+        west = jnp.where(to_west == k, parts[k][3], west)
+    lane = lax.broadcasted_iota(jnp.int32, cols_ref.shape, 1)
+    cols_ref[...] = jnp.where(lane < BS // 2, east, west)
+
+
+def combine(ocn, parts, rows):
+    ice = rows.shape[1]
     return pl.pallas_call(
         combine_kernel,
-        in_specs=[VM] * (len(parts) + 4),
-        out_specs=[VM, VM],
+        in_specs=[SM] + [VM] * (len(parts) + 1),
+        out_specs=[VM, VM, VM],
         out_shape=[
             jax.ShapeDtypeStruct((6, ice, BS), F32),
             jax.ShapeDtypeStruct((3, ice, BS), F32),
+            jax.ShapeDtypeStruct((ice, BS), F32),
         ],
+        compiler_params=params(2),
         name="combine",
-    )(*parts, u, wind, rate, strength)
-
-
-def solve_kernel(dst_ref, list_ref, me_ref, x_ref, rem_ref, w_hbm, *refs):
+    )(ocn, *parts, rows)
+
+
+def solve_kernel(dst_ref, list_ref, me_ref, x_ref, rem_ref, row0_ref, rown_ref, w_hbm, *refs):
     groups_n, _, ice, _ = x_ref.shape
     outs = refs[:groups_n]
     ice_ref, fin, flux, back, buf, sems = refs[groups_n:]
     entries = dst_ref.shape[0]
     per_block = entries // ice
-    nbl = outs[0].shape[1]
+    nbl = outs[0].shape[0] // 3
     count = list_ref[entries + UNROLL]
     groups = lax.div(count + UNROLL - 1, UNROLL)
 
@@ -412,17 +452,22 @@
         flux[r, 3:4, :] = jnp.zeros((1, BS), F32)
     loop()
     for k in range(groups_n):
-        outs[k][...] = back[:, k * nbl : (k + 1) * nbl, :]
-
-
-def solve(dst, lst, me, x, rem, weights, nbl):
+        for f in range(3):
+            outs[k][f * nbl : (f + 1) * nbl, :] = back[f, k * nbl : (k + 1) * nbl, :]
+    outs[1][3 * nbl :, :] = rown_ref[...]
+    outs[groups_n - 1][3 * nbl :, :] = row0_ref[...]
+
+
+def solve(dst, lst, me, x, rem, row0, rown, weights, nbl):
     groups_n, _, ice, _ = x.shape
-    chunk = jax.ShapeDtypeStruct((3, nbl, BS), F32)
+    assert groups_n > 2
+    extra = [row0.shape[0] if k in (1, groups_n - 1) else 0 for k in range(groups_n)]
+    chunks = [jax.ShapeDtypeStruct((3 * nbl + e, BS), F32) for e in extra]
     return pl.pallas_call(
         solve_kernel,
-        in_specs=[SM, SM, SM, VM, VM, ANY],
+        in_specs=[SM, SM, SM, VM, VM, VM, VM, ANY],
         out_specs=[VM] * (groups_n + 1),
-        out_shape=[chunk] * groups_n + [jax.ShapeDtypeStruct((2, ice * BS), F32)],
+        out_shape=chunks + [jax.ShapeDtypeStruct((2, ice * BS), F32)],
         scratch_shapes=[
             pltpu.VMEM((2, groups_n * ice, BS), F32),
             pltpu.VMEM((ice, 4, BS), F32),
@@ -430,9 +475,9 @@
             pltpu.VMEM((BWD_SLOTS, BS, BS), BF16),
             pltpu.SemaphoreType.DMA((BWD_SLOTS,)),
         ],
-        compiler_params=params(),
+        compiler_params=params(14),
         name="solve",
-    )(dst, lst, me, x, rem, weights)
+    )(dst, lst, me, x, rem, row0, rown, in_hbm(weights))
 
 
 def finish_kernel(*refs):
@@ -441,36 +486,30 @@
     height, across = t_ref.shape[2:]
     for f in range(3):
         for h in range(across // BS):
-            v = chunks[0][f, h * height : (h + 1) * height, :]
+            at = (f * (across // BS) + h) * height
+            v = chunks[0][at : at + height, :]
             for c in chunks[1:]:
-                v = v + c[f, h * height : (h + 1) * height, :]
+                v = v + c[at : at + height, :]
             flux_ref[f, :, h * BS : (h + 1) * BS] = v
     out_ref[0, 0] = t_ref[0, 0] + 0.5 * flux_ref[2]
 
 
 def finish(chunks, tracers_next):
     height, across = tracers_next.shape[2:]
-    whole = pl.BlockSpec(chunks[0].shape, lambda i: (0, 0, 0))
     level = pl.BlockSpec((1, 1, height, across), lambda i: (0, 0, 0, 0))
     return pl.pallas_call(
         finish_kernel,
         grid=(1,),
-        in_specs=[whole] * len(chunks) + [level],
+        in_specs=[VM] * len(chunks) + [level],
         out_specs=[pl.BlockSpec((3, height, across), lambda i: (0, 0, 0)), level],
         out_shape=[
             jax.ShapeDtypeStruct((3, height, across), F32),
             jax.ShapeDtypeStruct(tracers_next.shape, F32),
         ],
         input_output_aliases={len(chunks): 1},
+        compiler_params=params(4),
         name="finish",
     )(*chunks, tracers_next)
-
-
-def neighbours(low_edge, high_edge, axis):
-    n = lax.axis_size(axis)
-    up = [(i, i + 1) for i in range(n - 1)]
-    down = [(i + 1, i) for i in range(n - 1)]
-    return lax.ppermute(high_edge, axis, up), lax.ppermute(low_edge, axis, down)
 
 
 def coupled_step(
@@ -504,33 +543,28 @@
     code = jnp.where(mine, tile * (4 * nbl) + place, -1).reshape(-1)
     dst = (((tile - me) % n_grp) * nbl + place).reshape(-1)
 
-    row0, rown, col0, coln = pack_edges(tracers)
-    south, north = neighbours(row0, rown, "grp")
-    west, east = neighbours(col0, coln, "ocn")
-
-    surf = lax.all_gather(pack_surface(tracers, velocity), "grp", axis=0, tiled=True)
-    part, lst = forward(code, surf, weights, ice)
-    if n_ocn & (n_ocn - 1) == 0:
-        parts = [part]
-        for k in range(1, n_ocn):
-            parts.append(lax.ppermute(part, "ocn", [(i, i ^ k) for i in range(n_ocn)]))
-    else:
-        parts = [lax.psum(part, "ocn")]
-    x, rem = combine(
-        parts,
+    surf, lst = pack_surface(code, tracers, velocity)
+    surf = lax.all_gather(surf, "grp", axis=0, tiled=True)
+    part, row0, rown = forward(code, lst, surf, weights, tracers, ice)
+    assert n_ocn & (n_ocn - 1) == 0
+    parts = [part]
+    for k in range(1, n_ocn):
+        parts.append(lax.ppermute(part, "ocn", [(i, i ^ k) for i in range(n_ocn)]))
+    rows = ice_rows(
         ice_velocity,
         wind_stress,
         ice_mass_rate.reshape(ice, BS),
         ice_strength.reshape(ice, BS),
     )
+    x, rem, cols = combine(column.reshape(1), parts, rows)
     xg = lax.all_gather(x, "grp", axis=0)
-    *chunks, ice_final = solve(dst, lst, me.reshape(1), xg, rem, weights, nbl)
-    moved = [chunks[0]]
-    for k in range(1, n_grp):
+    *chunks, ice_final = solve(dst, lst, me.reshape(1), xg, rem, row0, rown, weights, nbl)
+    moved = {0: chunks[0]}
+    for k in [1, n_grp - 1] + list(range(2, n_grp - 1)):
         ring = [(i, (i + k) % n_grp) for i in range(n_grp)]
-        moved.append(lax.ppermute(chunks[k], "grp", ring))
-    tracers_next = stencil(tracers, velocity, north, south, east, west)
-    surface_flux, tracers_next = finish(moved, tracers_next)
+        moved[k] = lax.ppermute(chunks[k], "grp", ring)
+    tracers_next = stencil(me.reshape(1), n_grp, tracers, velocity, moved[1], moved[n_grp - 1], cols)
+    surface_flux, tracers_next = finish([moved[k] for k in range(n_grp)], tracers_next)
     return tracers_next, surface_flux, ice_final
 
 

time: 82.8 us -> 59.5 us (0.72)
  starting transfers between devices: 20.1 us -> 8.57 us
  Pallas kernels: 24.9 us -> 17.6 us
  local copies, waits for them, and re-layouts: 3.1 us -> 0.35 us
  blocking collectives: 21.7 us -> 20.8 us
    ppermute x11 -> x7, starting transfers between devices: 15.2 us -> 3.63 us  [coupled_step(): moved[k] = lax.ppermute(chunks[k], 'grp', ring)]
    pallas_call x7, Pallas kernels: 24.9 us -> 17.6 us  [the longest x1 5.84 us: solve(): pl.pallas_call(solve_kernel, in_specs=[SM, SM, SM, VM, VM, VM, VM, ANY],...]
    unnamed x34 -> x12, local copies, waits for them, and re-layouts: 2.77 us -> 0.02 us
    ppermute x11 -> x7, waiting for transfers between devices: 6.2 us -> 5.7 us  [coupled_step(): moved[k] = lax.ppermute(chunks[k], 'grp', ring)]
  transfers between devices with their start and end apart: 14 -> 10, of which waited for: 4 -> 6; matrix products, arithmetic and copies ran while one was open for 0% -> 0% of each run, Pallas kernels for 11% -> 6%
where the time goes in v1:
time: 59.5 us; the launch traced here: 58.8 us
  blocking collectives  20.8 us (35%)
  Pallas kernels  17.6 us (30%)
  waiting for transfers between devices  10 us (17%)
  starting transfers between devices  8.57 us (14%)
  between operations  0.73 us (1%)
  other arithmetic  0.72 us (1%)
    all_gather x1, blocking collectives, coupled_step(): surf = lax.all_gather(surf, 'grp', axis=0, tiled=True)  11.3 us
    all_gather x1, blocking collectives, coupled_step(): xg = lax.all_gather(x, 'grp', axis=0)  9.44 us
    pallas_call x1, Pallas kernels, solve(): pl.pallas_call(solve_kernel, in_specs=[SM, SM, SM, VM, VM, VM, VM, ANY],...  5.84 us
    ppermute x7, waiting for transfers between devices, coupled_step(): moved[k] = lax.ppermute(chunks[k], 'grp', ring)  5.7 us
    ppermute x3, starting transfers between devices, coupled_step(): parts.append(lax.ppermute(part, 'ocn', [(i, i ^ k) for i in range(n_ocn)]))  4.94 us
    pallas_call x1, Pallas kernels, forward(): pl.pallas_call(forward_kernel, in_specs=[SM, SM, VM, ANY, ANY], out_specs...  4.51 us
    ppermute x3, waiting for transfers between devices, coupled_step(): parts.append(lax.ppermute(part, 'ocn', [(i, i ^ k) for i in range(n_ocn)]))  4.35 us
    pallas_call x1, Pallas kernels, stencil(): pl.pallas_call(functools.partial(stencil_kernel, n_grp), grid=(levels //...  3.71 us
  transfers between devices with their start and end apart: 10, of which 6 were waited for; matrix products, arithmetic and copies ran while one was open for 0% of the time, Pallas kernels for 6%

profile of v1, /device:TPU:0, one launch (start us, length us, event | category | flops | bytes accessed | tf_op | source)
XLA Modules:
  0.0 58.8 jit_solution(15968939211669651316)
XLA Ops:
  0.6 0.7 %add_select_fusion.7 = (s32[32,8]{0,1:T(8,128)S(1)}, s32[32,8]{0,1:T(8,128)S(1)}) fusion(s32[32,8]{0,1:T(8,128)} %param.12, s32[]{:T(128)} %axis_index.25, s32[32]{0:T(128)} %param.13, s32[]{:T(128)} %axis_index.22), kind=kLoop, calls=%fused_computation.24 | loop fusion | flops 20224 | bytes 3208 | tf_op jit(solution)/shard_map/jit(_where)/select_n | solution.py:543
  1.4 0.1 copy.16
  1.4 0.1 reshape.30.code_ref
  1.5 2.0 %surface.1 = (bf16[4,64,128]{2,1,0:T(8,128)(2,1)S(1)}, s32[272]{0:T(512)S(1)}) custom-call(s32[256]{0:T(256)S(1)} %reshape.30.code_ref, f32[2,32,32,256]{3,2,1,0:T(8,128)} %dn_ref.1, f32[2,32,32,256]{3,2,1,0:T(8,128)} %v_ref.1), custom_call_target="tpu_custom_call" | custom-call | tf_op jit(solution)/shard_map/surface/pallas_call | solution.py:69
  3.5 11.3 %all_gather.9.surf_ref = bf16[32,64,128]{2,1,0:T(8,128)(2,1)S(1)} all-gather(bf16[4,64,128]{2,1,0:T(8,128)(2,1)S(1)} %get-tuple-element.23), channel_id=1, replica_groups=mesh['ocn'=4,'grp'=8] {'grp'}, dimensions={0}, use_global_device_ids=true | all-gather | bytes 589824 | tf_op jit(solution)/shard_map/all_gather | solution.py:547
  14.9 4.5 %forward.1 = (f32[4,32,128]{2,1,0:T(8,128)S(1)}, f32[128,128]{1,0:T(8,128)S(1)}, f32[128,128]{1,0:T(8,128)S(1)}) custom-call(s32[256]{0:T(256)S(1)} %reshape.30.code_ref, s32[272]{0:T(512)S(1)} %get-tuple-element.22.list_ref, bf16[32,64,128]{2,1,0:T(8,128)(2,1)S(1)} %all_gather.9.surf_ref, bf16[256,128,128]{2,1,0:T(8,128)(2,1)} %bitcast.9, ...), custom_call_target="tpu_custom_call" | custom-call | tf_op jit(solution)/shard_map/forward/pallas_call | solution.py:253
  19.4 4.3 %collective-permute-start.2 = (f32[4,32,128]{2,1,0:T(8,128)S(1)}, f32[4,32,128]{2,1,0:T(8,128)S(1)}, u32[]{:S(2)}, u32[]{:S(2)}) collective-permute-start(f32[4,32,128]{2,1,0:T(8,128)S(1)} %get-tuple-element.24.refs_0_), channel_id=1, source_target_pairs={{0,24},{8,16},{16,8},{24,0},{1,25},{9,17},{17,9},{25,1},{2,26},{10... | collective-permute-start | bytes 196616 | tf_op jit(solution)/shard_map/ppermute | solution.py:552
  23.7 0.6 %collective-permute-start = (f32[4,32,128]{2,1,0:T(8,128)S(1)}, f32[4,32,128]{2,1,0:T(8,128)S(1)}, u32[]{:S(2)}, u32[]{:S(2)}) collective-permute-start(f32[4,32,128]{2,1,0:T(8,128)S(1)} %get-tuple-element.24.refs_0_), channel_id=1, source_target_pairs={{0,8},{8,0},{16,24},{24,16},{1,9},{9,1},{17,25},{25,17},{2,10},{10... | collective-permute-start | bytes 196616 | tf_op jit(solution)/shard_map/ppermute | solution.py:552
  24.3 0.1 copy.15
  24.4 0.1 reshape.29.dst_ref
  24.6 1.5 %collective-permute-done.2.refs_3_ = f32[4,32,128]{2,1,0:T(8,128)S(1)} collective-permute-done((f32[4,32,128]{2,1,0:T(8,128)S(1)}, f32[4,32,128]{2,1,0:T(8,128)S(1)}, u32[]{:S(2)}, u32[]{:S(2)}) %collective-permute-start.2) | collective-permute-done | bytes 65568 | tf_op jit(solution)/shard_map/ppermute | solution.py:552
  26.1 2.8 %collective-permute-done.1.refs_2_ = f32[4,32,128]{2,1,0:T(8,128)S(1)} collective-permute-done((f32[4,32,128]{2,1,0:T(8,128)S(1)}, f32[4,32,128]{2,1,0:T(8,128)S(1)}, u32[]{:S(2)}, u32[]{:S(2)}) %collective-permute-start.1) | collective-permute-done | bytes 65568 | tf_op jit(solution)/shard_map/ppermute | solution.py:552
  28.9 0.1 collective-permute-done.refs_1_
  29.0 9.4 %all-gather = f32[48,32,128]{2,1,0:T(8,128)S(1)} all-gather(f32[6,32,128]{2,1,0:T(8,128)S(1)} %get-tuple-element.25), channel_id=2, replica_groups=mesh['ocn'=4,'grp'=8] {'grp'}, dimensions={0}, use_global_device_ids=true | all-gather | bytes 884736 | tf_op jit(solution)/shard_map/all_gather | solution.py:560
  38.4 5.8 %solve.1 = (f32[192,128]{1,0:T(8,128)S(1)}, f32[320,128]{1,0:T(8,128)S(1)}, f32[192,128]{1,0:T(8,128)S(1)}, f32[192,128]{1,0:T(8,128)S(1)}, f32[192,128]{1,0:T(8...) custom-call(s32[256]{0:T(256)S(1)} %reshape.29.dst_ref, ...), custom_call_target="tpu_custom_call" | custom-call | tf_op jit(solution)/shard_map/solve/pallas_call | solution.py:466
  44.3 0.1 collective-permute-start.3
  44.3 2.6 %collective-permute-start.9 = (f32[320,128]{1,0:T(8,128)S(1)}, f32[320,128]{1,0:T(8,128)S(1)}, u32[]{:S(2)}, u32[]{:S(2)}) collective-permute-start(f32[320,128]{1,0:T(8,128)S(1)} %get-tuple-element.36), channel_id=1, source_target_pairs={{0,7},{1,0},{2,1},{3,2},{4,3},{5,4},{6,5},{7,6},{8,15},{9,8},{10,9... | collective-permute-start | bytes 491528 | tf_op jit(solution)/shard_map/ppermute | solution.py:565
  47.0 0.8 %collective-permute-start.6 = (f32[192,128]{1,0:T(8,128)S(1)}, f32[192,128]{1,0:T(8,128)S(1)}, u32[]{:S(2)}, u32[]{:S(2)}) collective-permute-start(f32[192,128]{1,0:T(8,128)S(1)} %get-tuple-element.33), channel_id=1, source_target_pairs={{0,4},{1,5},{2,6},{3,7},{4,0},{5,1},{6,2},{7,3},{8,12},{9,13},{10,... | collective-permute-start | bytes 294920 | tf_op jit(solution)/shard_map/ppermute | solution.py:565
  47.7 3.9 %collective-permute-done.3.south_ref.refs_1_ = f32[320,128]{1,0:T(8,128)S(1)} collective-permute-done((f32[320,128]{1,0:T(8,128)S(1)}, f32[320,128]{1,0:T(8,128)S(1)}, u32[]{:S(2)}, u32[]{:S(2)}) %collective-permute-start.3) | collective-permute-done | bytes 163872 | tf_op jit(solution)/shard_map/ppermute | solution.py:565
  51.7 0.2 collective-permute-start.8
  51.8 3.7 %stencil.1.refs_8_ = f32[2,32,32,256]{3,2,1,0:T(8,128)} custom-call(s32[1]{0:T(128)} %bitcast.me_ref, f32[2,32,32,256]{3,2,1,0:T(8,128)S(1)} %copy-done, f32[2,32,32,256]{3,2,1,0:T(8,128)S(1)} %copy-done, f32[2,32,32,256]{3,2,1,0:T(8,128)S(1)} %copy-done, f32[2,32,32,256]{3,2,1,0:T(8,128)S(1)} %copy-done.1, ...), custom_call_target="tpu_custom_call" | custom-call | flops 120000000 | bytes 8388608 | tf_op jit(solution)/shard_map/stencil/pallas_call | solution.py:141
  55.6 0.8 %collective-permute-done.6.refs_4_ = f32[192,128]{1,0:T(8,128)S(1)} collective-permute-done((f32[192,128]{1,0:T(8,128)S(1)}, f32[192,128]{1,0:T(8,128)S(1)}, u32[]{:S(2)}, u32[]{:S(2)}) %collective-permute-start.6) | collective-permute-done | bytes 98336 | tf_op jit(solution)/shard_map/ppermute | solution.py:565
  56.4 1.0 %collective-permute-done.8.refs_6_ = f32[192,128]{1,0:T(8,128)S(1)} collective-permute-done((f32[192,128]{1,0:T(8,128)S(1)}, f32[192,128]{1,0:T(8,128)S(1)}, u32[]{:S(2)}, u32[]{:S(2)}) %collective-permute-start.8) | collective-permute-done | bytes 98336 | tf_op jit(solution)/shard_map/ppermute | solution.py:565
  57.3 1.5 %finish.1 = (f32[3,32,256]{2,1,0:T(8,128)}, f32[2,32,32,256]{3,2,1,0:T(8,128)}) custom-call(f32[192,128]{1,0:T(8,128)S(1)} %get-tuple-element.29.refs_0_, f32[320,128]{1,0:T(8,128)S(1)} %collective-permute-done.3.south_ref.refs_1_, f32[192,128]{1,0:T(8,128)S(1)} %collective-permute-done.4.refs_2_, ...), custom_call_target="tpu_custom_call", output_to_operand_aliasing={{1}: (8, {})} | custom-call | tf_op jit(solution)/shard_map/finish/pallas_call | solution.py:500
  (22 shorter events, 0.1 us)
Async XLA Ops:
  14.9 9.6 %copy-start.2 = (f32[2,4096]{1,0:T(2,128)S(1)}, f32[2,4096]{1,0:T(2,128)}, u32[]{:S(2)}) copy-start(f32[2,4096]{1,0:T(2,128)} %u_ref.1) | copy-start | bytes 98308
  14.9 9.6 %copy-start.3 = (f32[2,4096]{1,0:T(2,128)S(1)}, f32[2,4096]{1,0:T(2,128)}, u32[]{:S(2)}) copy-start(f32[2,4096]{1,0:T(2,128)} %wind_ref.1) | copy-start | bytes 98308
  14.9 9.7 %copy-start.4 = (f32[4096]{0:T(1024)S(1)}, f32[4096]{0:T(1024)}, u32[]{:S(2)}) copy-start(f32[4096]{0:T(1024)} %param.15) | copy-start | bytes 49156
  14.9 9.7 %copy-start.5 = (f32[4096]{0:T(1024)S(1)}, f32[4096]{0:T(1024)}, u32[]{:S(2)}) copy-start(f32[4096]{0:T(1024)} %param.16) | copy-start | bytes 49156
  19.4 6.7 %collective-permute-start.2 = (f32[4,32,128]{2,1,0:T(8,128)S(1)}, f32[4,32,128]{2,1,0:T(8,128)S(1)}, u32[]{:S(2)}, u32[]{:S(2)}) collective-permute-start(f32[4,32,128]{2,1,0:T(8,128)S(1)} %get-tuple-element.24.refs_0_), channel_id=1, source_target_pairs={{0,24},{8,16},{16,8},{24,0},{1,25},{9,17},{17,9},{25,1},{2,26},{10... | collective-permute-start | bytes 196616 | tf_op jit(solution)/shard_map/ppermute | solution.py:552
  23.7 5.2 %collective-permute-start.1 = (f32[4,32,128]{2,1,0:T(8,128)S(1)}, f32[4,32,128]{2,1,0:T(8,128)S(1)}, u32[]{:S(2)}, u32[]{:S(2)}) collective-permute-start(f32[4,32,128]{2,1,0:T(8,128)S(1)} %get-tuple-element.24.refs_0_), channel_id=1, source_target_pairs={{0,16},{8,24},{16,0},{24,8},{1,17},{9,25},{17,1},{25,9},{2,18},{10... | collective-permute-start | bytes 196616 | tf_op jit(solution)/shard_map/ppermute | solution.py:552
  23.7 5.3 %collective-permute-start = (f32[4,32,128]{2,1,0:T(8,128)S(1)}, f32[4,32,128]{2,1,0:T(8,128)S(1)}, u32[]{:S(2)}, u32[]{:S(2)}) collective-permute-start(f32[4,32,128]{2,1,0:T(8,128)S(1)} %get-tuple-element.24.refs_0_), channel_id=1, source_target_pairs={{0,8},{8,0},{16,24},{24,16},{1,9},{9,1},{17,25},{25,17},{2,10},{10... | collective-permute-start | bytes 196616 | tf_op jit(solution)/shard_map/ppermute | solution.py:552
  38.4 13.4 %copy-start = (f32[2,32,32,256]{3,2,1,0:T(8,128)S(1)}, f32[2,32,32,256]{3,2,1,0:T(8,128)}, u32[]{:S(2)}) copy-start(f32[2,32,32,256]{3,2,1,0:T(8,128)} %dn_ref.1) | copy-start | bytes 6291460
  38.4 13.4 %copy-start.1 = (f32[2,32,32,256]{3,2,1,0:T(8,128)S(1)}, f32[2,32,32,256]{3,2,1,0:T(8,128)}, u32[]{:S(2)}) copy-start(f32[2,32,32,256]{3,2,1,0:T(8,128)} %v_ref.1) | copy-start | bytes 6291460
  44.3 7.4 %collective-permute-start.3 = (f32[320,128]{1,0:T(8,128)S(1)}, f32[320,128]{1,0:T(8,128)S(1)}, u32[]{:S(2)}, u32[]{:S(2)}) collective-permute-start(f32[320,128]{1,0:T(8,128)S(1)} %get-tuple-element.30), channel_id=1, source_target_pairs={{0,1},{1,2},{2,3},{3,4},{4,5},{5,6},{6,7},{7,0},{8,9},{9,10},{10,1... | collective-permute-start | bytes 491528 | tf_op jit(solution)/shard_map/ppermute | solution.py:565
  44.3 7.3 %collective-permute-start.9 = (f32[320,128]{1,0:T(8,128)S(1)}, f32[320,128]{1,0:T(8,128)S(1)}, u32[]{:S(2)}, u32[]{:S(2)}) collective-permute-start(f32[320,128]{1,0:T(8,128)S(1)} %get-tuple-element.36), channel_id=1, source_target_pairs={{0,7},{1,0},{2,1},{3,2},{4,3},{5,4},{6,5},{7,6},{8,15},{9,8},{10,9... | collective-permute-start | bytes 491528 | tf_op jit(solution)/shard_map/ppermute | solution.py:565
  47.0 8.6 %collective-permute-start.4 = (f32[192,128]{1,0:T(8,128)S(1)}, f32[192,128]{1,0:T(8,128)S(1)}, u32[]{:S(2)}, u32[]{:S(2)}) collective-permute-start(f32[192,128]{1,0:T(8,128)S(1)} %get-tuple-element.31), channel_id=1, source_target_pairs={{0,2},{1,3},{2,4},{3,5},{4,6},{5,7},{6,0},{7,1},{8,10},{9,11},{10,... | collective-permute-start | bytes 294920 | tf_op jit(solution)/shard_map/ppermute | solution.py:565
  47.0 8.6 %collective-permute-start.5 = (f32[192,128]{1,0:T(8,128)S(1)}, f32[192,128]{1,0:T(8,128)S(1)}, u32[]{:S(2)}, u32[]{:S(2)}) collective-permute-start(f32[192,128]{1,0:T(8,128)S(1)} %get-tuple-element.32), channel_id=1, source_target_pairs={{0,3},{1,4},{2,5},{3,6},{4,7},{5,0},{6,1},{7,2},{8,11},{9,12},{10,... | collective-permute-start | bytes 294920 | tf_op jit(solution)/shard_map/ppermute | solution.py:565
  47.0 9.4 %collective-permute-start.6 = (f32[192,128]{1,0:T(8,128)S(1)}, f32[192,128]{1,0:T(8,128)S(1)}, u32[]{:S(2)}, u32[]{:S(2)}) collective-permute-start(f32[192,128]{1,0:T(8,128)S(1)} %get-tuple-element.33), channel_id=1, source_target_pairs={{0,4},{1,5},{2,6},{3,7},{4,0},{5,1},{6,2},{7,3},{8,12},{9,13},{10,... | collective-permute-start | bytes 294920 | tf_op jit(solution)/shard_map/ppermute | solution.py:565
  51.7 4.7 %collective-permute-start.7 = (f32[192,128]{1,0:T(8,128)S(1)}, f32[192,128]{1,0:T(8,128)S(1)}, u32[]{:S(2)}, u32[]{:S(2)}) collective-permute-start(f32[192,128]{1,0:T(8,128)S(1)} %get-tuple-element.34), channel_id=1, source_target_pairs={{0,5},{1,6},{2,7},{3,0},{4,1},{5,2},{6,3},{7,4},{8,13},{9,14},{10,... | collective-permute-start | bytes 294920 | tf_op jit(solution)/shard_map/ppermute | solution.py:565
  51.7 5.7 %collective-permute-start.8 = (f32[192,128]{1,0:T(8,128)S(1)}, f32[192,128]{1,0:T(8,128)S(1)}, u32[]{:S(2)}, u32[]{:S(2)}) collective-permute-start(f32[192,128]{1,0:T(8,128)S(1)} %get-tuple-element.35), channel_id=1, source_target_pairs={{0,6},{1,7},{2,0},{3,1},{4,2},{5,3},{6,4},{7,5},{8,14},{9,15},{10,... | collective-permute-start | bytes 294920 | tf_op jit(solution)/shard_map/ppermute | solution.py:565

commit v2 on v1

--- a/solution.py
+++ b/solution.py
@@ -84,7 +84,7 @@
 
 
 def stencil_kernel(
-    n_grp, me_ref, t_ref, up_ref, dn_ref, v_ref, south_ref, north_ref, cols_ref, out_ref
+    n_grp, me_ref, t_ref, up_ref, dn_ref, v_ref, south_ref, north_ref, cols_ref, out_ref, level_ref
 ):
     step = pl.program_id(0)
     steps = pl.num_programs(0)
@@ -122,12 +122,18 @@
             s = jnp.where(row == 0, south, pltpu.roll(x, 1, 0))
             n = jnp.where(row == height - 1, north, pltpu.roll(x, height - 1, 0))
             advect = u * (e - w) * 0.5 + v * (n - s) * 0.5
-            out_ref[t, i] = (
+            new = (
                 x
                 + 0.2 * (e + w + n + s - 4.0 * x)
                 - 0.5 * advect
                 + 0.2 * (above + below - 2.0 * x)
             )
+            out_ref[t, i] = new
+            if t == 0 and i == 0:
+
+                @pl.when(step == 0)
+                def _():
+                    level_ref[...] = new
 
 
 def stencil(me, n_grp, tracers, velocity, south, north, cols):
@@ -142,8 +148,11 @@
         functools.partial(stencil_kernel, n_grp),
         grid=(levels // lc,),
         in_specs=[SM, main, up, dn, main, VM, VM, VM],
-        out_specs=main,
-        out_shape=jax.ShapeDtypeStruct(tracers.shape, F32),
+        out_specs=[main, pl.BlockSpec((height, across), lambda i: (0, 0))],
+        out_shape=[
+            jax.ShapeDtypeStruct(tracers.shape, F32),
+            jax.ShapeDtypeStruct((height, across), F32),
+        ],
         compiler_params=params(14),
         cost_estimate=pl.CostEstimate(
             flops=120_000_000, bytes_accessed=4 * tracers.size * 4, transcendentals=0
@@ -186,9 +195,15 @@
     return start, loop
 
 
-def forward_kernel(
-    code_ref, list_ref, surf_ref, w_hbm, t_hbm, out_ref, row0_ref, rown_ref, rows, acc, tiles, buf, sems, t_sem
-):
+def edge_partners(n):
+    return [k for k in range(1, n) if k & (k + 1) == 0]
+
+
+def forward_kernel(n_ocn, code_ref, list_ref, ocn_ref, surf_ref, w_hbm, tiles, *refs):
+    ks = edge_partners(n_ocn)
+    out_ref, row0_ref, rown_ref = refs[:3]
+    sends = refs[3 : 3 + len(ks)]
+    rows, acc, buf, sems = refs[3 + len(ks) :]
     entries = code_ref.shape[0]
     ice = acc.shape[0]
     per_block = entries // ice
@@ -215,8 +230,6 @@
 
     start, loop = stream_weights(list_ref, groups, w_hbm, buf, sems, compute)
     start()
-    whole = pltpu.make_async_copy(t_hbm, tiles, t_sem)
-    whole.start()
     planes = surf_ref.shape[0]
     for p in range(planes):
         rows[p * nbl : (p + 1) * nbl, :] = surf_ref[p].astype(F32)
@@ -224,12 +237,11 @@
     loop()
     for r in range(ice):
         a = acc[r]
-        out_ref[0, r : r + 1, :] = 0.5 * (-0.05 * a[1:2] - a[0:1])
-        out_ref[1, r : r + 1, :] = a[2:3]
-        out_ref[2, r : r + 1, :] = a[3:4]
+        out_ref[r : r + 1, :] = 0.5 * (-0.05 * a[1:2] - a[0:1])
+        out_ref[ice + r : ice + r + 1, :] = a[2:3]
+        out_ref[2 * ice + r : 2 * ice + r + 1, :] = a[3:4]
 
     _, levels, height, across = tiles.shape
-    whole.wait()
     lane = lax.broadcasted_iota(jnp.int32, (height, BS), 1)
     cols = jnp.zeros((height, BS), F32)
     for t in range(2):
@@ -242,30 +254,38 @@
                 at = h * 2 * levels + c
                 row0_ref[at : at + 1, :] = tiles[t, i, 0:1, h * BS : (h + 1) * BS]
                 rown_ref[at : at + 1, :] = tiles[t, i, height - 1 : height, h * BS : (h + 1) * BS]
-    out_ref[3] = cols
-
-
-def forward(code, lst, surf, weights, tracers, ice):
+    half = height // 2
+    side = lane[:half] < BS // 2
+    turned = pltpu.roll(cols, BS // 2, 1)
+    low = jnp.where(side, cols[:half], turned[half:])
+    high = jnp.where(side, turned[:half], cols[half:])
+    me = ocn_ref[0]
+    for k, send in zip(ks, sends):
+        send[0 : 3 * ice, :] = out_ref[...]
+        send[3 * ice :, :] = jnp.where((me ^ k) == me + 1, high, low)
+
+
+def forward(code, lst, ocn, n_ocn, surf, weights, tracers, ice):
     planes, nbl = surf.shape[:2]
     _, levels, height, across = tracers.shape
     assert 4 * levels == BS and height == ice
     edge = jax.ShapeDtypeStruct((2 * levels * (across // BS), BS), F32)
+    ks = edge_partners(n_ocn)
+    send = jax.ShapeDtypeStruct((3 * ice + height // 2, BS), F32)
     return pl.pallas_call(
-        forward_kernel,
-        in_specs=[SM, SM, VM, ANY, ANY],
-        out_specs=[VM, VM, VM],
-        out_shape=[jax.ShapeDtypeStruct((4, ice, BS), F32), edge, edge],
+        functools.partial(forward_kernel, n_ocn),
+        in_specs=[SM, SM, SM, VM, ANY, VM],
+        out_specs=[VM] * (3 + len(ks)),
+        out_shape=[jax.ShapeDtypeStruct((3 * ice, BS), F32), edge, edge] + [send] * len(ks),
         scratch_shapes=[
             pltpu.VMEM((planes * nbl, BS), F32),
             pltpu.VMEM((ice, 4, BS), F32),
-            pltpu.VMEM(tracers.shape, F32),
             pltpu.VMEM((FWD_SLOTS, BS, BS), BF16),
             pltpu.SemaphoreType.DMA((FWD_SLOTS,)),
-            pltpu.SemaphoreType.DMA(()),
         ],
         compiler_params=params(12),
         name="forward",
-    )(code, lst, surf, in_hbm(weights), in_hbm(tracers))
+    )(code, lst, ocn, surf, in_hbm(weights), tracers)
 
 
 def icerows_kernel(u_ref, wind_ref, rate_ref, strength_ref, x_ref):
@@ -296,20 +316,24 @@
     parts = refs[:-4]
     rows_ref, x_ref, rem_ref, cols_ref = refs[-4:]
     me, n = ocn_ref[0], len(parts)
-    vals = [p[0:3] for p in parts]
+    ice = rem_ref.shape[1]
+    vals = [[p[c * ice : (c + 1) * ice, :] for c in range(3)] for p in parts]
     while len(vals) > 1:
-        vals = [a + b for a, b in zip(vals[0::2], vals[1::2])]
-    rem_ref[...] = vals[0]
+        vals = [[x + y for x, y in zip(a, b)] for a, b in zip(vals[0::2], vals[1::2])]
     x_ref[...] = rows_ref[...]
+    for c in range(3):
+        rem_ref[c] = vals[0][c]
     for c in range(2):
         x_ref[c] = rows_ref[c] + vals[0][1 + c]
     to_east = jnp.where(me < n - 1, me ^ (me + 1), 0)
     to_west = jnp.where(me > 0, me ^ (me - 1), 0)
-    east = jnp.zeros(cols_ref.shape, F32)
+    east = jnp.zeros((cols_ref.shape[0] // 2, BS), F32)
     west = east
-    for k in range(1, n):
-        east = jnp.where(to_east == k, parts[k][3], east)
-        west = jnp.where(to_west == k, parts[k][3], west)
+    for k in edge_partners(n):
+        east = jnp.where(to_east == k, parts[k][3 * ice :, :], east)
+        west = jnp.where(to_west == k, parts[k][3 * ice :, :], west)
+    east = jnp.concatenate([east, pltpu.roll(east, BS // 2, 1)], axis=0)
+    west = jnp.concatenate([pltpu.roll(west, BS // 2, 1), west], axis=0)
     lane = lax.broadcasted_iota(jnp.int32, cols_ref.shape, 1)
     cols_ref[...] = jnp.where(lane < BS // 2, east, west)
 
@@ -364,26 +388,27 @@
     base = [plane(0), plane(1)]
     current = [plane(2), plane(3)]
     rate1 = plane(4) + 1.0
-    half_strength = 0.5 * plane(5)
+    strength = plane(5)
+    strength2 = 2.0 * strength
     lane = lax.broadcasted_iota(jnp.int32, (n_rows, BS), 1)
-    row = lax.broadcasted_iota(jnp.int32, (n_rows, BS), 0)
+    corner = lax.broadcasted_iota(jnp.int32, (8, BS), 0) * BS + lane[:8]
 
     def picard(u):
         left, right = [], []
         for z in u:
             a = pltpu.roll(z, 1, 1)
-            b = pltpu.roll(a, 1, 0)
-            b = jnp.where(row == 0, 0.0, b)
-            left.append(jnp.where(lane == 0, b, a))
+            a = jnp.where(lane == 0, pltpu.roll(a, 1, 0), a)
+            left.append(jnp.concatenate([jnp.where(corner == 0, 0.0, a[:8]), a[8:]], axis=0))
             a = pltpu.roll(z, BS - 1, 1)
-            b = pltpu.roll(a, n_rows - 1, 0)
-            b = jnp.where(row == n_rows - 1, 0.0, b)
-            right.append(jnp.where(lane == BS - 1, b, a))
-        sx = 0.5 * (right[0] - left[0])
-        sy = 0.5 * (right[1] - left[1])
-        zeta = half_strength / jnp.sqrt(sx * sx + sy * sy + 0.25)
-        den = 1.0 / (rate1 + 2.0 * zeta)
-        return [(base[c] + zeta * (left[c] + right[c])) * den for c in range(2)]
+            a = jnp.where(lane == BS - 1, pltpu.roll(a, n_rows - 1, 0), a)
+            end = jnp.where(corner == 8 * BS - 1, 0.0, a[n_rows - 8 :])
+            right.append(jnp.concatenate([a[: n_rows - 8], end], axis=0))
+        dx = right[0] - left[0]
+        dy = right[1] - left[1]
+        d = dx * dx + dy * dy + 1.0
+        q = d * lax.rsqrt(d)
+        inverse = 1.0 / (rate1 * q + strength2)
+        return [(base[c] * q + strength * (left[c] + right[c])) * inverse for c in range(2)]
 
     def dot(a, b):
         return jnp.sum(a[0] * b[0] + a[1] * b[1], keepdims=True) / total
@@ -481,35 +506,40 @@
 
 
 def finish_kernel(*refs):
-    chunks = refs[:-3]
-    t_ref, flux_ref, out_ref = refs[-3:]
-    height, across = t_ref.shape[2:]
-    for f in range(3):
+    chunks = refs[:-6]
+    level_ref, _, flux_ref, out_hbm, buf, sem = refs[-6:]
+    height, across = level_ref.shape
+    put = pltpu.make_async_copy(buf, out_hbm.at[0, 0], sem)
+    for f in (2, 0, 1):
         for h in range(across // BS):
             at = (f * (across // BS) + h) * height
             v = chunks[0][at : at + height, :]
             for c in chunks[1:]:
                 v = v + c[at : at + height, :]
             flux_ref[f, :, h * BS : (h + 1) * BS] = v
-    out_ref[0, 0] = t_ref[0, 0] + 0.5 * flux_ref[2]
-
-
-def finish(chunks, tracers_next):
-    height, across = tracers_next.shape[2:]
-    level = pl.BlockSpec((1, 1, height, across), lambda i: (0, 0, 0, 0))
+            if f == 2:
+                cols = slice(h * BS, (h + 1) * BS)
+                buf[:, cols] = level_ref[:, cols] + 0.5 * v
+        if f == 2:
+            put.start()
+    put.wait()
+
+
+def finish(chunks, level, tracers_next):
+    height, across = level.shape
     return pl.pallas_call(
         finish_kernel,
-        grid=(1,),
-        in_specs=[VM] * len(chunks) + [level],
-        out_specs=[pl.BlockSpec((3, height, across), lambda i: (0, 0, 0)), level],
+        in_specs=[VM] * (len(chunks) + 1) + [ANY],
+        out_specs=[VM, ANY],
         out_shape=[
             jax.ShapeDtypeStruct((3, height, across), F32),
             jax.ShapeDtypeStruct(tracers_next.shape, F32),
         ],
-        input_output_aliases={len(chunks): 1},
+        scratch_shapes=[pltpu.VMEM((height, across), F32), pltpu.SemaphoreType.DMA(())],
+        input_output_aliases={len(chunks) + 1: 1},
         compiler_params=params(4),
         name="finish",
-    )(*chunks, tracers_next)
+    )(*chunks, level, in_hbm(tracers_next))
 
 
 def coupled_step(
@@ -545,26 +575,29 @@
 
     surf, lst = pack_surface(code, tracers, velocity)
     surf = lax.all_gather(surf, "grp", axis=0, tiled=True)
-    part, row0, rown = forward(code, lst, surf, weights, tracers, ice)
     assert n_ocn & (n_ocn - 1) == 0
+    ocn = column.reshape(1)
+    part, row0, rown, *sends = forward(code, lst, ocn, n_ocn, surf, weights, tracers, ice)
+    sends = dict(zip(edge_partners(n_ocn), sends))
     parts = [part]
     for k in range(1, n_ocn):
-        parts.append(lax.ppermute(part, "ocn", [(i, i ^ k) for i in range(n_ocn)]))
+        pairs = [(i, i ^ k) for i in range(n_ocn)]
+        parts.append(lax.ppermute(sends.get(k, part), "ocn", pairs))
     rows = ice_rows(
         ice_velocity,
         wind_stress,
         ice_mass_rate.reshape(ice, BS),
         ice_strength.reshape(ice, BS),
     )
-    x, rem, cols = combine(column.reshape(1), parts, rows)
+    x, rem, cols = combine(ocn, parts, rows)
     xg = lax.all_gather(x, "grp", axis=0)
     *chunks, ice_final = solve(dst, lst, me.reshape(1), xg, rem, row0, rown, weights, nbl)
     moved = {0: chunks[0]}
     for k in [1, n_grp - 1] + list(range(2, n_grp - 1)):
         ring = [(i, (i + k) % n_grp) for i in range(n_grp)]
         moved[k] = lax.ppermute(chunks[k], "grp", ring)
-    tracers_next = stencil(me.reshape(1), n_grp, tracers, velocity, moved[1], moved[n_grp - 1], cols)
-    surface_flux, tracers_next = finish([moved[k] for k in range(n_grp)], tracers_next)
+    tracers_next, level = stencil(me.reshape(1), n_grp, tracers, velocity, moved[1], moved[n_grp - 1], cols)
+    surface_flux, tracers_next = finish([moved[k] for k in range(n_grp)], level, tracers_next)
     return tracers_next, surface_flux, ice_final
 
 

time: 59.5 us -> 59.1 us (level)
  transfers between devices with their start and end apart: 10 -> 10, of which waited for: 6 -> 4; matrix products, arithmetic and copies ran while one was open for 0% -> 0% of each run, Pallas kernels for 6% -> 7%
where the time goes in v2:
time: 59.1 us; the launch traced here: 58.4 us
  blocking collectives  20.9 us (35%)
  Pallas kernels  17.6 us (30%)
  waiting for transfers between devices  9.63 us (16%)
  starting transfers between devices  8.5 us (14%)
  between operations  0.74 us (1%)
  other arithmetic  0.72 us (1%)
    all_gather x1, blocking collectives, coupled_step(): surf = lax.all_gather(surf, 'grp', axis=0, tiled=True)  11.3 us
    all_gather x1, blocking collectives, coupled_step(): xg = lax.all_gather(x, 'grp', axis=0)  9.58 us
    pallas_call x1, Pallas kernels, solve(): pl.pallas_call(solve_kernel, in_specs=[SM, SM, SM, VM, VM, VM, VM, ANY],...  5.65 us
    ppermute x7, waiting for transfers between devices, coupled_step(): moved[k] = lax.ppermute(chunks[k], 'grp', ring)  5.38 us
    ppermute x3, starting transfers between devices, coupled_step(): parts.append(lax.ppermute(sends.get(k, part), 'ocn', pairs))  4.84 us
    pallas_call x1, Pallas kernels, forward(): pl.pallas_call(functools.partial(forward_kernel, n_ocn), in_specs=[SM, SM...  4.39 us
    ppermute x3, waiting for transfers between devices, coupled_step(): parts.append(lax.ppermute(sends.get(k, part), 'ocn', pairs))  4.25 us
    pallas_call x1, Pallas kernels, stencil(): pl.pallas_call(functools.partial(stencil_kernel, n_grp), grid=(levels //...  4.02 us
  transfers between devices with their start and end apart: 10, of which 4 were waited for; matrix products, arithmetic and copies ran while one was open for 0% of the time, Pallas kernels for 7%

profile of v2, /device:TPU:0, one launch (start us, length us, event | category | flops | bytes accessed | tf_op | source)
XLA Modules:
  0.0 58.4 jit_solution(12022610481761750508)
XLA Ops:
  0.6 0.7 %add_select_fusion.7 = (s32[32,8]{0,1:T(8,128)S(1)}, s32[32,8]{0,1:T(8,128)S(1)}) fusion(s32[32,8]{0,1:T(8,128)} %param.12, s32[]{:T(128)} %axis_index.25, s32[32]{0:T(128)} %param.13, s32[]{:T(128)} %axis_index.22), kind=kLoop, calls=%fused_computation.24 | loop fusion | flops 20224 | bytes 3208 | tf_op jit(solution)/shard_map/jit(_where)/select_n | solution.py:573
  1.4 0.1 copy.16
  1.4 0.1 reshape.30.code_ref
  1.5 2.1 %surface.1 = (bf16[4,64,128]{2,1,0:T(8,128)(2,1)S(1)}, s32[272]{0:T(512)S(1)}) custom-call(s32[256]{0:T(256)S(1)} %reshape.30.code_ref, f32[2,32,32,256]{3,2,1,0:T(8,128)} %dn_ref.1, f32[2,32,32,256]{3,2,1,0:T(8,128)} %v_ref.1), custom_call_target="tpu_custom_call" | custom-call | tf_op jit(solution)/shard_map/surface/pallas_call | solution.py:69
  3.6 11.3 %all_gather.9.surf_ref = bf16[32,64,128]{2,1,0:T(8,128)(2,1)S(1)} all-gather(bf16[4,64,128]{2,1,0:T(8,128)(2,1)S(1)} %get-tuple-element.27), channel_id=1, replica_groups=mesh['ocn'=4,'grp'=8] {'grp'}, dimensions={0}, use_global_device_ids=true | all-gather | bytes 589824 | tf_op jit(solution)/shard_map/all_gather | solution.py:577
  15.0 4.4 %forward.1 = (f32[96,128]{1,0:T(8,128)S(1)}, f32[128,128]{1,0:T(8,128)S(1)}, f32[128,128]{1,0:T(8,128)S(1)}, f32[112,128]{1,0:T(8,128)S(1)}, f32[112,128]{1,0:T(8,128)S(1)}) custom-call(s32[256]{0:T(256)S(1)} %reshape.30.code_ref, s32[272]{0:T(512)S(1)} %get-tuple-element.26.list_ref, s32[1]{0:T(128)} %bitcast.1.ocn_ref, ...), custom_call_target="tpu_custom_call" | custom-call | tf_op jit(solution)/shard_map/forward/pallas_call | solution.py:275
  19.4 1.9 %collective-permute-start = (f32[112,128]{1,0:T(8,128)S(1)}, f32[112,128]{1,0:T(8,128)S(1)}, u32[]{:S(2)}, u32[]{:S(2)}) collective-permute-start(f32[112,128]{1,0:T(8,128)S(1)} %get-tuple-element.29), channel_id=1, source_target_pairs={{0,8},{8,0},{16,24},{24,16},{1,9},{9,1},{17,25},{25,17},{2,10},{10... | collective-permute-start | bytes 172040 | tf_op jit(solution)/shard_map/ppermute | solution.py:585
  21.2 2.5 %collective-permute-start.2 = (f32[112,128]{1,0:T(8,128)S(1)}, f32[112,128]{1,0:T(8,128)S(1)}, u32[]{:S(2)}, u32[]{:S(2)}) collective-permute-start(f32[112,128]{1,0:T(8,128)S(1)} %get-tuple-element.30), channel_id=1, source_target_pairs={{0,24},{8,16},{16,8},{24,0},{1,25},{9,17},{17,9},{25,1},{2,26},{10... | collective-permute-start | bytes 172040 | tf_op jit(solution)/shard_map/ppermute | solution.py:585
  23.7 0.5 collective-permute-start.1
  24.2 0.1 copy.15
  24.3 0.1 reshape.29.dst_ref
  24.5 4.2 %collective-permute-done.1.refs_2_ = f32[96,128]{1,0:T(8,128)S(1)} collective-permute-done((f32[96,128]{1,0:T(8,128)S(1)}, f32[96,128]{1,0:T(8,128)S(1)}, u32[]{:S(2)}, u32[]{:S(2)}) %collective-permute-start.1) | collective-permute-done | bytes 49184 | tf_op jit(solution)/shard_map/ppermute | solution.py:585
  28.7 0.1 combine.1
  28.8 9.6 %all-gather = f32[48,32,128]{2,1,0:T(8,128)S(1)} all-gather(f32[6,32,128]{2,1,0:T(8,128)S(1)} %get-tuple-element.31), channel_id=2, replica_groups=mesh['ocn'=4,'grp'=8] {'grp'}, dimensions={0}, use_global_device_ids=true | all-gather | bytes 884736 | tf_op jit(solution)/shard_map/all_gather | solution.py:593
  38.4 5.7 %solve.1 = (f32[192,128]{1,0:T(8,128)S(1)}, f32[320,128]{1,0:T(8,128)S(1)}, f32[192,128]{1,0:T(8,128)S(1)}, f32[192,128]{1,0:T(8,128)S(1)}, f32[192,128]{1,0:T(8...) custom-call(s32[256]{0:T(256)S(1)} %reshape.29.dst_ref, ...), custom_call_target="tpu_custom_call" | custom-call | tf_op jit(solution)/shard_map/solve/pallas_call | solution.py:491
  44.1 0.1 collective-permute-start.3
  44.1 2.6 %collective-permute-start.9 = (f32[320,128]{1,0:T(8,128)S(1)}, f32[320,128]{1,0:T(8,128)S(1)}, u32[]{:S(2)}, u32[]{:S(2)}) collective-permute-start(f32[320,128]{1,0:T(8,128)S(1)} %get-tuple-element.42), channel_id=1, source_target_pairs={{0,7},{1,0},{2,1},{3,2},{4,3},{5,4},{6,5},{7,6},{8,15},{9,8},{10,9... | collective-permute-start | bytes 491528 | tf_op jit(solution)/shard_map/ppermute | solution.py:598
  46.8 0.8 %collective-permute-start.6 = (f32[192,128]{1,0:T(8,128)S(1)}, f32[192,128]{1,0:T(8,128)S(1)}, u32[]{:S(2)}, u32[]{:S(2)}) collective-permute-start(f32[192,128]{1,0:T(8,128)S(1)} %get-tuple-element.39), channel_id=1, source_target_pairs={{0,4},{1,5},{2,6},{3,7},{4,0},{5,1},{6,2},{7,3},{8,12},{9,13},{10,... | collective-permute-start | bytes 294920 | tf_op jit(solution)/shard_map/ppermute | solution.py:598
  47.5 3.9 %collective-permute-done.3.south_ref.refs_1_ = f32[320,128]{1,0:T(8,128)S(1)} collective-permute-done((f32[320,128]{1,0:T(8,128)S(1)}, f32[320,128]{1,0:T(8,128)S(1)}, u32[]{:S(2)}, u32[]{:S(2)}) %collective-permute-start.3) | collective-permute-done | bytes 163872 | tf_op jit(solution)/shard_map/ppermute | solution.py:598
  51.5 0.2 collective-permute-start.8
  51.7 4.0 %stencil.1 = (f32[2,32,32,256]{3,2,1,0:T(8,128)}, f32[32,256]{1,0:T(8,128)S(1)}) custom-call(s32[1]{0:T(128)} %bitcast.me_ref, f32[2,32,32,256]{3,2,1,0:T(8,128)S(1)} %copy-done, f32[2,32,32,256]{3,2,1,0:T(8,128)S(1)} %copy-done, f32[2,32,32,256]{3,2,1,0:T(8,128)S(1)} %copy-done, f32[2,32,32,256]{3,2,1,0:T(8,128)S(1)} %copy-done.1, ...), custom_call_target="tpu_custom_call" | custom-call | flops 120000000 | bytes 8388608 | tf_op jit(solution)/shard_map/stencil/pallas_call | solution.py:147
  55.7 0.5 collective-permute-done.6.refs_4_
  56.2 1.0 %collective-permute-done.8.refs_6_ = f32[192,128]{1,0:T(8,128)S(1)} collective-permute-done((f32[192,128]{1,0:T(8,128)S(1)}, f32[192,128]{1,0:T(8,128)S(1)}, u32[]{:S(2)}, u32[]{:S(2)}) %collective-permute-start.8) | collective-permute-done | bytes 98336 | tf_op jit(solution)/shard_map/ppermute | solution.py:598
  57.1 1.3 %finish.1 = (f32[3,32,256]{2,1,0:T(8,128)}, f32[2,32,32,256]{3,2,1,0:T(8,128)}) custom-call(f32[192,128]{1,0:T(8,128)S(1)} %get-tuple-element.35.refs_0_, f32[320,128]{1,0:T(8,128)S(1)} %collective-permute-done.3.south_ref.refs_1_, f32[192,128]{1,0:T(8,128)S(1)} %collective-permute-done.4.refs_2_, ...), custom_call_target="tpu_custom_call", output_to_operand_aliasing={{1}: (9, {})} | custom-call | tf_op jit(solution)/shard_map/finish/pallas_call | solution.py:530
  (22 shorter events, 0.1 us)
Async XLA Ops:
  1.5 13.4 %copy-start = (f32[2,32,32,256]{3,2,1,0:T(8,128)S(1)}, f32[2,32,32,256]{3,2,1,0:T(8,128)}, u32[]{:S(2)}) copy-start(f32[2,32,32,256]{3,2,1,0:T(8,128)} %dn_ref.1) | copy-start | bytes 6291460
  15.0 9.4 %copy-start.2 = (f32[2,4096]{1,0:T(2,128)S(1)}, f32[2,4096]{1,0:T(2,128)}, u32[]{:S(2)}) copy-start(f32[2,4096]{1,0:T(2,128)} %u_ref.1) | copy-start | bytes 98308
  15.0 9.4 %copy-start.3 = (f32[2,4096]{1,0:T(2,128)S(1)}, f32[2,4096]{1,0:T(2,128)}, u32[]{:S(2)}) copy-start(f32[2,4096]{1,0:T(2,128)} %wind_ref.1) | copy-start | bytes 98308
  15.0 9.4 %copy-start.4 = (f32[4096]{0:T(1024)S(1)}, f32[4096]{0:T(1024)}, u32[]{:S(2)}) copy-start(f32[4096]{0:T(1024)} %param.15) | copy-start | bytes 49156
  15.0 9.4 %copy-start.5 = (f32[4096]{0:T(1024)S(1)}, f32[4096]{0:T(1024)}, u32[]{:S(2)}) copy-start(f32[4096]{0:T(1024)} %param.16) | copy-start | bytes 49156
  19.4 9.4 %collective-permute-start = (f32[112,128]{1,0:T(8,128)S(1)}, f32[112,128]{1,0:T(8,128)S(1)}, u32[]{:S(2)}, u32[]{:S(2)}) collective-permute-start(f32[112,128]{1,0:T(8,128)S(1)} %get-tuple-element.29), channel_id=1, source_target_pairs={{0,8},{8,0},{16,24},{24,16},{1,9},{9,1},{17,25},{25,17},{2,10},{10... | collective-permute-start | bytes 172040 | tf_op jit(solution)/shard_map/ppermute | solution.py:585
  21.2 7.5 %collective-permute-start.2 = (f32[112,128]{1,0:T(8,128)S(1)}, f32[112,128]{1,0:T(8,128)S(1)}, u32[]{:S(2)}, u32[]{:S(2)}) collective-permute-start(f32[112,128]{1,0:T(8,128)S(1)} %get-tuple-element.30), channel_id=1, source_target_pairs={{0,24},{8,16},{16,8},{24,0},{1,25},{9,17},{17,9},{25,1},{2,26},{10... | collective-permute-start | bytes 172040 | tf_op jit(solution)/shard_map/ppermute | solution.py:585
  23.7 5.0 %collective-permute-start.1 = (f32[96,128]{1,0:T(8,128)S(1)}, f32[96,128]{1,0:T(8,128)S(1)}, u32[]{:S(2)}, u32[]{:S(2)}) collective-permute-start(f32[96,128]{1,0:T(8,128)S(1)} %get-tuple-element.28.refs_0_), channel_id=1, source_target_pairs={{0,16},{8,24},{16,0},{24,8},{1,17},{9,25},{17,1},{25,9},{2,18},{10... | collective-permute-start | bytes 147464 | tf_op jit(solution)/shard_map/ppermute | solution.py:585
  38.4 13.3 %copy-start.1 = (f32[2,32,32,256]{3,2,1,0:T(8,128)S(1)}, f32[2,32,32,256]{3,2,1,0:T(8,128)}, u32[]{:S(2)}) copy-start(f32[2,32,32,256]{3,2,1,0:T(8,128)} %v_ref.1) | copy-start | bytes 6291460
  44.1 7.4 %collective-permute-start.3 = (f32[320,128]{1,0:T(8,128)S(1)}, f32[320,128]{1,0:T(8,128)S(1)}, u32[]{:S(2)}, u32[]{:S(2)}) collective-permute-start(f32[320,128]{1,0:T(8,128)S(1)} %get-tuple-element.36), channel_id=1, source_target_pairs={{0,1},{1,2},{2,3},{3,4},{4,5},{5,6},{6,7},{7,0},{8,9},{9,10},{10,1... | collective-permute-start | bytes 491528 | tf_op jit(solution)/shard_map/ppermute | solution.py:598
  44.1 7.3 %collective-permute-start.9 = (f32[320,128]{1,0:T(8,128)S(1)}, f32[320,128]{1,0:T(8,128)S(1)}, u32[]{:S(2)}, u32[]{:S(2)}) collective-permute-start(f32[320,128]{1,0:T(8,128)S(1)} %get-tuple-element.42), channel_id=1, source_target_pairs={{0,7},{1,0},{2,1},{3,2},{4,3},{5,4},{6,5},{7,6},{8,15},{9,8},{10,9... | collective-permute-start | bytes 491528 | tf_op jit(solution)/shard_map/ppermute | solution.py:598
  46.8 8.9 %collective-permute-start.4 = (f32[192,128]{1,0:T(8,128)S(1)}, f32[192,128]{1,0:T(8,128)S(1)}, u32[]{:S(2)}, u32[]{:S(2)}) collective-permute-start(f32[192,128]{1,0:T(8,128)S(1)} %get-tuple-element.37), channel_id=1, source_target_pairs={{0,2},{1,3},{2,4},{3,5},{4,6},{5,7},{6,0},{7,1},{8,10},{9,11},{10,... | collective-permute-start | bytes 294920 | tf_op jit(solution)/shard_map/ppermute | solution.py:598
  46.8 8.9 %collective-permute-start.5 = (f32[192,128]{1,0:T(8,128)S(1)}, f32[192,128]{1,0:T(8,128)S(1)}, u32[]{:S(2)}, u32[]{:S(2)}) collective-permute-start(f32[192,128]{1,0:T(8,128)S(1)} %get-tuple-element.38), channel_id=1, source_target_pairs={{0,3},{1,4},{2,5},{3,6},{4,7},{5,0},{6,1},{7,2},{8,11},{9,12},{10,... | collective-permute-start | bytes 294920 | tf_op jit(solution)/shard_map/ppermute | solution.py:598
  46.8 9.4 %collective-permute-start.6 = (f32[192,128]{1,0:T(8,128)S(1)}, f32[192,128]{1,0:T(8,128)S(1)}, u32[]{:S(2)}, u32[]{:S(2)}) collective-permute-start(f32[192,128]{1,0:T(8,128)S(1)} %get-tuple-element.39), channel_id=1, source_target_pairs={{0,4},{1,5},{2,6},{3,7},{4,0},{5,1},{6,2},{7,3},{8,12},{9,13},{10,... | collective-permute-start | bytes 294920 | tf_op jit(solution)/shard_map/ppermute | solution.py:598
  51.5 4.7 %collective-permute-start.7 = (f32[192,128]{1,0:T(8,128)S(1)}, f32[192,128]{1,0:T(8,128)S(1)}, u32[]{:S(2)}, u32[]{:S(2)}) collective-permute-start(f32[192,128]{1,0:T(8,128)S(1)} %get-tuple-element.40), channel_id=1, source_target_pairs={{0,5},{1,6},{2,7},{3,0},{4,1},{5,2},{6,3},{7,4},{8,13},{9,14},{10,... | collective-permute-start | bytes 294920 | tf_op jit(solution)/shard_map/ppermute | solution.py:598
  51.5 5.7 %collective-permute-start.8 = (f32[192,128]{1,0:T(8,128)S(1)}, f32[192,128]{1,0:T(8,128)S(1)}, u32[]{:S(2)}, u32[]{:S(2)}) collective-permute-start(f32[192,128]{1,0:T(8,128)S(1)} %get-tuple-element.41), channel_id=1, source_target_pairs={{0,6},{1,7},{2,0},{3,1},{4,2},{5,3},{6,4},{7,5},{8,14},{9,15},{10,... | collective-permute-start | bytes 294920 | tf_op jit(solution)/shard_map/ppermute | solution.py:598

commit v3 on v2

--- a/solution.py
+++ b/solution.py
@@ -31,9 +31,26 @@
     return pltpu.CompilerParams(vmem_limit_bytes=mib * 1024 * 1024)
 
 
-def surface_kernel(code_ref, t_hbm, v_hbm, out_ref, list_ref, buf, sems):
+def split(v, d):
+    if d & (d - 1) == 0:
+        return lax.shift_right_logical(v, d.bit_length() - 1), v & (d - 1)
+    return lax.div(v, d), lax.rem(v, d)
+
+
+def place_of(local, height, halves):
+    tile, j = split(local, height * halves)
+    row, half = split(j, halves)
+    return tile, half * height + row
+
+
+def surface_kernel(
+    n_grp, blocks_ref, count_ref, ocn_ref, t_hbm, v_hbm, out_ref, list_ref, buf, sems
+):
     height, across = buf.shape[1:]
-    entries = code_ref.shape[0]
+    per_block, ice = blocks_ref.shape
+    room = ice * per_block + UNROLL
+    size = n_grp * height * across // BS
+    lowest = ocn_ref[0] * size
     copies = [
         pltpu.make_async_copy(
             (t_hbm if f < 2 else v_hbm).at[f % 2, 0], buf.at[f], sems.at[f]
@@ -43,17 +60,20 @@
     for c in copies:
         c.start()
 
-    def scan(i, n):
-        for q in range(8):
-            e = i * 8 + q
-            list_ref[n] = e
-            n = n + jnp.where(code_ref[e] >= 0, 1, 0)
+    def scan(r, n):
+        live = count_ref[r]
+        for k in range(per_block):
+            local = blocks_ref[k, r] - lowest
+            list_ref[n] = r * per_block + k
+            list_ref[room + n] = local
+            n = n + jnp.where((local >= 0) & (local < size) & (k < live), 1, 0)
         return n
 
-    count = lax.fori_loop(0, entries // 8, scan, 0)
+    count = lax.fori_loop(0, ice, scan, 0)
     for q in range(UNROLL):
         list_ref[count + q] = 0
-    list_ref[entries + UNROLL] = count
+        list_ref[room + count + q] = 0
+    list_ref[2 * room] = count
     for c in copies:
         c.wait()
     for f in range(4):
@@ -63,16 +83,16 @@
             ].astype(BF16)
 
 
-def pack_surface(code, tracers, velocity):
+def pack_surface(n_grp, blocks, count, ocn, tracers, velocity):
     height, across = tracers.shape[2:]
     nbl = height * across // BS
     return pl.pallas_call(
-        surface_kernel,
-        in_specs=[SM, ANY, ANY],
+        functools.partial(surface_kernel, n_grp),
+        in_specs=[SM, SM, SM, ANY, ANY],
         out_specs=[VM, SM],
         out_shape=[
             jax.ShapeDtypeStruct((4, nbl, BS), BF16),
-            jax.ShapeDtypeStruct((code.shape[0] + UNROLL + 8,), jnp.int32),
+            jax.ShapeDtypeStruct((2 * (blocks.size + UNROLL) + 8,), jnp.int32),
         ],
         scratch_shapes=[
             pltpu.VMEM((4, height, across), F32),
@@ -80,7 +100,7 @@
         ],
         compiler_params=params(4),
         name="surface",
-    )(code, in_hbm(tracers), in_hbm(velocity))
+    )(in_hbm(blocks), in_hbm(count), ocn, in_hbm(tracers), in_hbm(velocity))
 
 
 def stencil_kernel(
@@ -199,23 +219,26 @@
     return [k for k in range(1, n) if k & (k + 1) == 0]
 
 
-def forward_kernel(n_ocn, code_ref, list_ref, ocn_ref, surf_ref, w_hbm, tiles, *refs):
+def forward_kernel(n_ocn, list_ref, ocn_ref, surf_ref, w_hbm, tiles, *refs):
     ks = edge_partners(n_ocn)
     out_ref, row0_ref, rown_ref = refs[:3]
     sends = refs[3 : 3 + len(ks)]
     rows, acc, buf, sems = refs[3 + len(ks) :]
-    entries = code_ref.shape[0]
+    entries = w_hbm.shape[0]
+    room = entries + UNROLL
     ice = acc.shape[0]
     per_block = entries // ice
     nbl = surf_ref.shape[1]
-    count = list_ref[entries + UNROLL]
+    halves = nbl // tiles.shape[2]
+    count = list_ref[2 * room]
     groups = lax.div(count + UNROLL - 1, UNROLL)
     first = lax.broadcasted_iota(jnp.int32, (4, BS), 0)
 
     def compute(base, slot):
         for q in range(UNROLL):
             e = list_ref[base + q]
-            at = jnp.maximum(code_ref[e], 0)
+            tile, place = place_of(list_ref[room + base + q], nbl // halves, halves)
+            at = tile * (4 * nbl) + place
             r0 = jnp.broadcast_to(rows[pl.ds(at, 1), :], (4, BS))
             r1 = jnp.broadcast_to(rows[pl.ds(at + nbl, 1), :], (4, BS))
             r2 = jnp.broadcast_to(rows[pl.ds(at + 2 * nbl, 1), :], (4, BS))
@@ -265,7 +288,7 @@
         send[3 * ice :, :] = jnp.where((me ^ k) == me + 1, high, low)
 
 
-def forward(code, lst, ocn, n_ocn, surf, weights, tracers, ice):
+def forward(lst, ocn, n_ocn, surf, weights, tracers, ice):
     planes, nbl = surf.shape[:2]
     _, levels, height, across = tracers.shape
     assert 4 * levels == BS and height == ice
@@ -274,7 +297,7 @@
     send = jax.ShapeDtypeStruct((3 * ice + height // 2, BS), F32)
     return pl.pallas_call(
         functools.partial(forward_kernel, n_ocn),
-        in_specs=[SM, SM, SM, VM, ANY, VM],
+        in_specs=[SM, SM, VM, ANY, VM],
         out_specs=[VM] * (3 + len(ks)),
         out_shape=[jax.ShapeDtypeStruct((3 * ice, BS), F32), edge, edge] + [send] * len(ks),
         scratch_shapes=[
@@ -285,7 +308,7 @@
         ],
         compiler_params=params(12),
         name="forward",
-    )(code, lst, ocn, surf, in_hbm(weights), tracers)
+    )(lst, ocn, surf, in_hbm(weights), tracers)
 
 
 def icerows_kernel(u_ref, wind_ref, rate_ref, strength_ref, x_ref):
@@ -354,14 +377,15 @@
     )(ocn, *parts, rows)
 
 
-def solve_kernel(dst_ref, list_ref, me_ref, x_ref, rem_ref, row0_ref, rown_ref, w_hbm, *refs):
+def solve_kernel(halves, list_ref, me_ref, x_ref, rem_ref, row0_ref, rown_ref, w_hbm, *refs):
     groups_n, _, ice, _ = x_ref.shape
     outs = refs[:groups_n]
     ice_ref, fin, flux, back, buf, sems = refs[groups_n:]
-    entries = dst_ref.shape[0]
+    entries = w_hbm.shape[0]
+    room = entries + UNROLL
     per_block = entries // ice
     nbl = outs[0].shape[0] // 3
-    count = list_ref[entries + UNROLL]
+    count = list_ref[2 * room]
     groups = lax.div(count + UNROLL - 1, UNROLL)
 
     def compute(base, slot):
@@ -371,7 +395,9 @@
             part = lax.dot_general(
                 s, buf[slot + q], (((1,), (0,)), ((), ())), preferred_element_type=F32
             )
-            at = dst_ref[e]
+            tile, place = place_of(list_ref[room + base + q], nbl // halves, halves)
+            k = tile - me_ref[0]
+            at = jnp.where(k < 0, k + groups_n, k) * nbl + place
             for f in range(3):
                 back[f, pl.ds(at, 1), :] = back[f, pl.ds(at, 1), :] + part[f : f + 1]
 
@@ -483,14 +509,14 @@
     outs[groups_n - 1][3 * nbl :, :] = row0_ref[...]
 
 
-def solve(dst, lst, me, x, rem, row0, rown, weights, nbl):
+def solve(lst, me, x, rem, row0, rown, weights, nbl, halves):
     groups_n, _, ice, _ = x.shape
     assert groups_n > 2
     extra = [row0.shape[0] if k in (1, groups_n - 1) else 0 for k in range(groups_n)]
     chunks = [jax.ShapeDtypeStruct((3 * nbl + e, BS), F32) for e in extra]
     return pl.pallas_call(
-        solve_kernel,
-        in_specs=[SM, SM, SM, VM, VM, VM, VM, ANY],
+        functools.partial(solve_kernel, halves),
+        in_specs=[SM, SM, VM, VM, VM, VM, ANY],
         out_specs=[VM] * (groups_n + 1),
         out_shape=chunks + [jax.ShapeDtypeStruct((2, ice * BS), F32)],
         scratch_shapes=[
@@ -502,7 +528,7 @@
         ],
         compiler_params=params(14),
         name="solve",
-    )(dst, lst, me, x, rem, row0, rown, in_hbm(weights))
+    )(lst, me, x, rem, row0, rown, in_hbm(weights))
 
 
 def finish_kernel(*refs):
@@ -563,21 +589,11 @@
     ice, per_block = remap_blocks.shape
     weights = remap_weights.reshape(ice * per_block, BS, BS)
 
-    local = remap_blocks % (n_grp * nbl)
-    tile = local // nbl
-    j = local % nbl
-    place = (j % halves) * height + j // halves
-    mine = (jnp.arange(per_block)[None, :] < remap_count[:, None]) & (
-        remap_blocks // (n_grp * nbl) == column
-    )
-    code = jnp.where(mine, tile * (4 * nbl) + place, -1).reshape(-1)
-    dst = (((tile - me) % n_grp) * nbl + place).reshape(-1)
-
-    surf, lst = pack_surface(code, tracers, velocity)
+    ocn = column.reshape(1)
+    surf, lst = pack_surface(n_grp, remap_blocks.T, remap_count, ocn, tracers, velocity)
     surf = lax.all_gather(surf, "grp", axis=0, tiled=True)
     assert n_ocn & (n_ocn - 1) == 0
-    ocn = column.reshape(1)
-    part, row0, rown, *sends = forward(code, lst, ocn, n_ocn, surf, weights, tracers, ice)
+    part, row0, rown, *sends = forward(lst, ocn, n_ocn, surf, weights, tracers, ice)
     sends = dict(zip(edge_partners(n_ocn), sends))
     parts = [part]
     for k in range(1, n_ocn):
@@ -591,7 +607,9 @@
     )
     x, rem, cols = combine(ocn, parts, rows)
     xg = lax.all_gather(x, "grp", axis=0)
-    *chunks, ice_final = solve(dst, lst, me.reshape(1), xg, rem, row0, rown, weights, nbl)
+    *chunks, ice_final = solve(
+        lst, me.reshape(1), xg, rem, row0, rown, weights, nbl, halves
+    )
     moved = {0: chunks[0]}
     for k in [1, n_grp - 1] + list(range(2, n_grp - 1)):
         ring = [(i, (i + k) % n_grp) for i in range(n_grp)]

time: 59.1 us -> 59 us (level)
  Pallas kernels: 17.6 us -> 18.4 us
  other arithmetic: 0.72 us -> 0 us
    pallas_call x2, Pallas kernels: 7.73 us -> 8.56 us  [the longest x1 5.67 us: solve(): pl.pallas_call(functools.partial(solve_kernel, halves), in_specs=[SM, SM,...]
    select_n x1 -> x0, other arithmetic: 0.72 us -> none  [coupled_step(): code = jnp.where(mine, tile * (4 * nbl) + place, -1).reshape(-1)]
where the time goes in v3:
time: 59 us; the launch traced here: 58.4 us
  blocking collectives  20.9 us (35%)
  Pallas kernels  18.4 us (31%)
  waiting for transfers between devices  9.85 us (17%)
  starting transfers between devices  8.5 us (14%)
  between operations  0.71 us (1%)
    all_gather x1, blocking collectives, coupled_step(): surf = lax.all_gather(surf, 'grp', axis=0, tiled=True)  11.3 us
    all_gather x1, blocking collectives, coupled_step(): xg = lax.all_gather(x, 'grp', axis=0)  9.56 us
    pallas_call x1, Pallas kernels, solve(): pl.pallas_call(functools.partial(solve_kernel, halves), in_specs=[SM, SM,...  5.67 us
    ppermute x7, waiting for transfers between devices, coupled_step(): moved[k] = lax.ppermute(chunks[k], 'grp', ring)  5.41 us
    ppermute x3, starting transfers between devices, coupled_step(): parts.append(lax.ppermute(sends.get(k, part), 'ocn', pairs))  4.87 us
    ppermute x3, waiting for transfers between devices, coupled_step(): parts.append(lax.ppermute(sends.get(k, part), 'ocn', pairs))  4.44 us
    pallas_call x1, Pallas kernels, forward(): pl.pallas_call(functools.partial(forward_kernel, n_ocn), in_specs=[SM, SM...  4.39 us
    pallas_call x1, Pallas kernels, stencil(): pl.pallas_call(functools.partial(stencil_kernel, n_grp), grid=(levels //...  4.01 us
  transfers between devices with their start and end apart: 10, of which 4 were waited for; matrix products, arithmetic and copies ran while one was open for 0% of the time, Pallas kernels for 7%

profile of v3, /device:TPU:0, one launch (start us, length us, event | category | flops | bytes accessed | tf_op | source)
XLA Modules:
  0.0 58.4 jit_solution(4600221730215659547)
XLA Ops:
  0.6 2.9 %surface.1 = (bf16[4,64,128]{2,1,0:T(8,128)(2,1)S(1)}, s32[536]{0:T(1024)S(1)}) custom-call(s32[8,32]{1,0:T(8,128)} %bitcast.12, s32[32]{0:T(128)} %count_ref.1, s32[1]{0:T(128)} %bitcast.1.ocn_ref, f32[2,32,32,256]{3,2,1,0:T(8,128)} %dn_ref.1, f32[2,32,32,256]{3,2,1,0:T(8,128)} %v_ref.1), custom_call_target="tpu_custom_call" | custom-call | tf_op jit(solution)/shard_map/surface/pallas_call | solution.py:89
  3.5 11.3 %all_gather.9.surf_ref = bf16[32,64,128]{2,1,0:T(8,128)(2,1)S(1)} all-gather(bf16[4,64,128]{2,1,0:T(8,128)(2,1)S(1)} %get-tuple-element.27), channel_id=1, replica_groups=mesh['ocn'=4,'grp'=8] {'grp'}, dimensions={0}, use_global_device_ids=true | all-gather | bytes 589824 | tf_op jit(solution)/shard_map/all_gather | solution.py:594
  14.9 0.0 copy-start.5
  14.9 4.4 %forward.1 = (f32[96,128]{1,0:T(8,128)S(1)}, f32[128,128]{1,0:T(8,128)S(1)}, f32[128,128]{1,0:T(8,128)S(1)}, f32[112,128]{1,0:T(8,128)S(1)}, f32[112,128]{1,0:T(8,128)S(1)}) custom-call(s32[536]{0:T(1024)S(1)} %get-tuple-element.26.list_ref, s32[1]{0:T(128)} %bitcast.1.ocn_ref, bf16[32,64,128]{2,1,0:T(8,128)(2,1)S(1)} %all_gather.9.surf_ref, ...), custom_call_target="tpu_custom_call" | custom-call | tf_op jit(solution)/shard_map/forward/pallas_call | solution.py:298
  19.3 1.9 %collective-permute-start = (f32[112,128]{1,0:T(8,128)S(1)}, f32[112,128]{1,0:T(8,128)S(1)}, u32[]{:S(2)}, u32[]{:S(2)}) collective-permute-start(f32[112,128]{1,0:T(8,128)S(1)} %get-tuple-element.29), channel_id=1, source_target_pairs={{0,8},{8,0},{16,24},{24,16},{1,9},{9,1},{17,25},{25,17},{2,10},{10... | collective-permute-start | bytes 172040 | tf_op jit(solution)/shard_map/ppermute | solution.py:601
  21.2 2.5 %collective-permute-start.2 = (f32[112,128]{1,0:T(8,128)S(1)}, f32[112,128]{1,0:T(8,128)S(1)}, u32[]{:S(2)}, u32[]{:S(2)}) collective-permute-start(f32[112,128]{1,0:T(8,128)S(1)} %get-tuple-element.30), channel_id=1, source_target_pairs={{0,24},{8,16},{16,8},{24,0},{1,25},{9,17},{17,9},{25,1},{2,26},{10... | collective-permute-start | bytes 172040 | tf_op jit(solution)/shard_map/ppermute | solution.py:601
  23.7 0.5 collective-permute-start.1
  24.2 0.1 icerows.1.refs_4_
  24.2 4.4 %collective-permute-done.1.refs_2_ = f32[96,128]{1,0:T(8,128)S(1)} collective-permute-done((f32[96,128]{1,0:T(8,128)S(1)}, f32[96,128]{1,0:T(8,128)S(1)}, u32[]{:S(2)}, u32[]{:S(2)}) %collective-permute-start.1) | collective-permute-done | bytes 49184 | tf_op jit(solution)/shard_map/ppermute | solution.py:601
  28.7 0.0 collective-permute-done.refs_1_
  28.7 0.1 combine.1
  28.8 9.6 %all-gather = f32[48,32,128]{2,1,0:T(8,128)S(1)} all-gather(f32[6,32,128]{2,1,0:T(8,128)S(1)} %get-tuple-element.31), channel_id=2, replica_groups=mesh['ocn'=4,'grp'=8] {'grp'}, dimensions={0}, use_global_device_ids=true | all-gather | bytes 884736 | tf_op jit(solution)/shard_map/all_gather | solution.py:609
  38.3 5.7 %solve.1 = (f32[192,128]{1,0:T(8,128)S(1)}, f32[320,128]{1,0:T(8,128)S(1)}, f32[192,128]{1,0:T(8,128)S(1)}, f32[192,128]{1,0:T(8,128)S(1)}, f32[192,128]{1,0:T(8...) custom-call(s32[536]{0:T(1024)S(1)} %get-tuple-element.26.list_ref, ...), custom_call_target="tpu_custom_call" | custom-call | tf_op jit(solution)/shard_map/solve/pallas_call | solution.py:517
  44.0 0.1 collective-permute-start.3
  44.1 2.6 %collective-permute-start.9 = (f32[320,128]{1,0:T(8,128)S(1)}, f32[320,128]{1,0:T(8,128)S(1)}, u32[]{:S(2)}, u32[]{:S(2)}) collective-permute-start(f32[320,128]{1,0:T(8,128)S(1)} %get-tuple-element.42), channel_id=1, source_target_pairs={{0,7},{1,0},{2,1},{3,2},{4,3},{5,4},{6,5},{7,6},{8,15},{9,8},{10,9... | collective-permute-start | bytes 491528 | tf_op jit(solution)/shard_map/ppermute | solution.py:616
  46.7 0.8 %collective-permute-start.6 = (f32[192,128]{1,0:T(8,128)S(1)}, f32[192,128]{1,0:T(8,128)S(1)}, u32[]{:S(2)}, u32[]{:S(2)}) collective-permute-start(f32[192,128]{1,0:T(8,128)S(1)} %get-tuple-element.39), channel_id=1, source_target_pairs={{0,4},{1,5},{2,6},{3,7},{4,0},{5,1},{6,2},{7,3},{8,12},{9,13},{10,... | collective-permute-start | bytes 294920 | tf_op jit(solution)/shard_map/ppermute | solution.py:616
  47.5 3.9 %collective-permute-done.3.south_ref.refs_1_ = f32[320,128]{1,0:T(8,128)S(1)} collective-permute-done((f32[320,128]{1,0:T(8,128)S(1)}, f32[320,128]{1,0:T(8,128)S(1)}, u32[]{:S(2)}, u32[]{:S(2)}) %collective-permute-start.3) | collective-permute-done | bytes 163872 | tf_op jit(solution)/shard_map/ppermute | solution.py:616
  51.4 0.0 collective-permute-start.7
  51.4 0.0 collective-permute-done.9.north_ref.refs_7_
  51.4 0.2 collective-permute-start.8
  51.6 4.0 %stencil.1 = (f32[2,32,32,256]{3,2,1,0:T(8,128)}, f32[32,256]{1,0:T(8,128)S(1)}) custom-call(s32[1]{0:T(128)} %bitcast.2.me_ref, f32[2,32,32,256]{3,2,1,0:T(8,128)S(1)} %copy-done, f32[2,32,32,256]{3,2,1,0:T(8,128)S(1)} %copy-done, f32[2,32,32,256]{3,2,1,0:T(8,128)S(1)} %copy-done, f32[2,32,32,256]{3,2,1,0:T(8,128)S(1)} %copy-done.1, ...), custom_call_target="tpu_custom_call" | custom-call | flops 120000000 | bytes 8388608 | tf_op jit(solution)/shard_map/stencil/pallas_call | solution.py:167
  55.6 0.5 collective-permute-done.6.refs_4_
  56.1 1.0 %collective-permute-done.8.refs_6_ = f32[192,128]{1,0:T(8,128)S(1)} collective-permute-done((f32[192,128]{1,0:T(8,128)S(1)}, f32[192,128]{1,0:T(8,128)S(1)}, u32[]{:S(2)}, u32[]{:S(2)}) %collective-permute-start.8) | collective-permute-done | bytes 98336 | tf_op jit(solution)/shard_map/ppermute | solution.py:616
  57.1 1.3 %finish.1 = (f32[3,32,256]{2,1,0:T(8,128)}, f32[2,32,32,256]{3,2,1,0:T(8,128)}) custom-call(f32[192,128]{1,0:T(8,128)S(1)} %get-tuple-element.35.refs_0_, f32[320,128]{1,0:T(8,128)S(1)} %collective-permute-done.3.south_ref.refs_1_, f32[192,128]{1,0:T(8,128)S(1)} %collective-permute-done.4.refs_2_, ...), custom_call_target="tpu_custom_call", output_to_operand_aliasing={{1}: (9, {})} | custom-call | tf_op jit(solution)/shard_map/finish/pallas_call | solution.py:556
  (17 shorter events, 0.0 us)
Async XLA Ops:
  0.6 14.2 %copy-start = (f32[2,32,32,256]{3,2,1,0:T(8,128)S(1)}, f32[2,32,32,256]{3,2,1,0:T(8,128)}, u32[]{:S(2)}) copy-start(f32[2,32,32,256]{3,2,1,0:T(8,128)} %dn_ref.1) | copy-start | bytes 6291460
  14.9 9.3 %copy-start.2 = (f32[2,4096]{1,0:T(2,128)S(1)}, f32[2,4096]{1,0:T(2,128)}, u32[]{:S(2)}) copy-start(f32[2,4096]{1,0:T(2,128)} %u_ref.1) | copy-start | bytes 98308
  14.9 9.3 %copy-start.3 = (f32[2,4096]{1,0:T(2,128)S(1)}, f32[2,4096]{1,0:T(2,128)}, u32[]{:S(2)}) copy-start(f32[2,4096]{1,0:T(2,128)} %wind_ref.1) | copy-start | bytes 98308
  14.9 9.3 %copy-start.4 = (f32[4096]{0:T(1024)S(1)}, f32[4096]{0:T(1024)}, u32[]{:S(2)}) copy-start(f32[4096]{0:T(1024)} %param.15) | copy-start | bytes 49156
  14.9 9.3 %copy-start.5 = (f32[4096]{0:T(1024)S(1)}, f32[4096]{0:T(1024)}, u32[]{:S(2)}) copy-start(f32[4096]{0:T(1024)} %param.16) | copy-start | bytes 49156
  19.3 9.4 %collective-permute-start = (f32[112,128]{1,0:T(8,128)S(1)}, f32[112,128]{1,0:T(8,128)S(1)}, u32[]{:S(2)}, u32[]{:S(2)}) collective-permute-start(f32[112,128]{1,0:T(8,128)S(1)} %get-tuple-element.29), channel_id=1, source_target_pairs={{0,8},{8,0},{16,24},{24,16},{1,9},{9,1},{17,25},{25,17},{2,10},{10... | collective-permute-start | bytes 172040 | tf_op jit(solution)/shard_map/ppermute | solution.py:601
  21.2 7.5 %collective-permute-start.2 = (f32[112,128]{1,0:T(8,128)S(1)}, f32[112,128]{1,0:T(8,128)S(1)}, u32[]{:S(2)}, u32[]{:S(2)}) collective-permute-start(f32[112,128]{1,0:T(8,128)S(1)} %get-tuple-element.30), channel_id=1, source_target_pairs={{0,24},{8,16},{16,8},{24,0},{1,25},{9,17},{17,9},{25,1},{2,26},{10... | collective-permute-start | bytes 172040 | tf_op jit(solution)/shard_map/ppermute | solution.py:601
  23.7 5.0 %collective-permute-start.1 = (f32[96,128]{1,0:T(8,128)S(1)}, f32[96,128]{1,0:T(8,128)S(1)}, u32[]{:S(2)}, u32[]{:S(2)}) collective-permute-start(f32[96,128]{1,0:T(8,128)S(1)} %get-tuple-element.28.refs_0_), channel_id=1, source_target_pairs={{0,16},{8,24},{16,0},{24,8},{1,17},{9,25},{17,1},{25,9},{2,18},{10... | collective-permute-start | bytes 147464 | tf_op jit(solution)/shard_map/ppermute | solution.py:601
  38.3 13.3 %copy-start.1 = (f32[2,32,32,256]{3,2,1,0:T(8,128)S(1)}, f32[2,32,32,256]{3,2,1,0:T(8,128)}, u32[]{:S(2)}) copy-start(f32[2,32,32,256]{3,2,1,0:T(8,128)} %v_ref.1) | copy-start | bytes 6291460
  44.0 7.4 %collective-permute-start.3 = (f32[320,128]{1,0:T(8,128)S(1)}, f32[320,128]{1,0:T(8,128)S(1)}, u32[]{:S(2)}, u32[]{:S(2)}) collective-permute-start(f32[320,128]{1,0:T(8,128)S(1)} %get-tuple-element.36), channel_id=1, source_target_pairs={{0,1},{1,2},{2,3},{3,4},{4,5},{5,6},{6,7},{7,0},{8,9},{9,10},{10,1... | collective-permute-start | bytes 491528 | tf_op jit(solution)/shard_map/ppermute | solution.py:616
  44.1 7.3 %collective-permute-start.9 = (f32[320,128]{1,0:T(8,128)S(1)}, f32[320,128]{1,0:T(8,128)S(1)}, u32[]{:S(2)}, u32[]{:S(2)}) collective-permute-start(f32[320,128]{1,0:T(8,128)S(1)} %get-tuple-element.42), channel_id=1, source_target_pairs={{0,7},{1,0},{2,1},{3,2},{4,3},{5,4},{6,5},{7,6},{8,15},{9,8},{10,9... | collective-permute-start | bytes 491528 | tf_op jit(solution)/shard_map/ppermute | solution.py:616
  46.7 8.9 %collective-permute-start.4 = (f32[192,128]{1,0:T(8,128)S(1)}, f32[192,128]{1,0:T(8,128)S(1)}, u32[]{:S(2)}, u32[]{:S(2)}) collective-permute-start(f32[192,128]{1,0:T(8,128)S(1)} %get-tuple-element.37), channel_id=1, source_target_pairs={{0,2},{1,3},{2,4},{3,5},{4,6},{5,7},{6,0},{7,1},{8,10},{9,11},{10,... | collective-permute-start | bytes 294920 | tf_op jit(solution)/shard_map/ppermute | solution.py:616
  46.7 8.9 %collective-permute-start.5 = (f32[192,128]{1,0:T(8,128)S(1)}, f32[192,128]{1,0:T(8,128)S(1)}, u32[]{:S(2)}, u32[]{:S(2)}) collective-permute-start(f32[192,128]{1,0:T(8,128)S(1)} %get-tuple-element.38), channel_id=1, source_target_pairs={{0,3},{1,4},{2,5},{3,6},{4,7},{5,0},{6,1},{7,2},{8,11},{9,12},{10,... | collective-permute-start | bytes 294920 | tf_op jit(solution)/shard_map/ppermute | solution.py:616
  46.7 9.4 %collective-permute-start.6 = (f32[192,128]{1,0:T(8,128)S(1)}, f32[192,128]{1,0:T(8,128)S(1)}, u32[]{:S(2)}, u32[]{:S(2)}) collective-permute-start(f32[192,128]{1,0:T(8,128)S(1)} %get-tuple-element.39), channel_id=1, source_target_pairs={{0,4},{1,5},{2,6},{3,7},{4,0},{5,1},{6,2},{7,3},{8,12},{9,13},{10,... | collective-permute-start | bytes 294920 | tf_op jit(solution)/shard_map/ppermute | solution.py:616
  51.4 4.7 %collective-permute-start.7 = (f32[192,128]{1,0:T(8,128)S(1)}, f32[192,128]{1,0:T(8,128)S(1)}, u32[]{:S(2)}, u32[]{:S(2)}) collective-permute-start(f32[192,128]{1,0:T(8,128)S(1)} %get-tuple-element.40), channel_id=1, source_target_pairs={{0,5},{1,6},{2,7},{3,0},{4,1},{5,2},{6,3},{7,4},{8,13},{9,14},{10,... | collective-permute-start | bytes 294920 | tf_op jit(solution)/shard_map/ppermute | solution.py:616
  51.4 5.7 %collective-permute-start.8 = (f32[192,128]{1,0:T(8,128)S(1)}, f32[192,128]{1,0:T(8,128)S(1)}, u32[]{:S(2)}, u32[]{:S(2)}) collective-permute-start(f32[192,128]{1,0:T(8,128)S(1)} %get-tuple-element.41), channel_id=1, source_target_pairs={{0,6},{1,7},{2,0},{3,1},{4,2},{5,3},{6,4},{7,5},{8,14},{9,15},{10,... | collective-permute-start | bytes 294920 | tf_op jit(solution)/shard_map/ppermute | solution.py:616
